TPU v7x, 32 devices: a whole 2x2x4 slice. The times are simulated.
32 devices in a mesh: dp: 8 (over z, x), mp: 4 (over y, core).
Axes of the slice: x: 2, y: 2, z: 4, core: 2. Of those that a mesh axis runs over, the one named last changes fastest.
Arguments:
- gradients: bfloat16 [8, 2, 4096, 1024], P('dp', None, None, 'mp'), may hold values from -6912 to 6912
- layer_mask: int32 [8, 2], P('dp'), may hold values from 0 to 1, as said below
- exit_losses: float32 [8, 2], P('dp'), may hold values from 1 to 24
- exit_weights: int32 [2], replicated, may hold values from 1 to 8
- params: float32 [2, 4096, 1024], P(None, 'dp', 'mp'), may hold values from -0.3 to 0.3
- moment: float32 [2, 4096, 1024], P(None, 'dp', 'mp'), may hold values from -6 to 6
- second: float32 [2, 4096, 1024], P(None, 'dp', 'mp'), may hold values from 0.5 to 4
Outputs:
- new_params: float32 [2, 4096, 1024], P(None, 'dp', 'mp')
- new_moment: float32 [2, 4096, 1024], P(None, 'dp', 'mp')
- new_second: float32 [2, 4096, 1024], P(None, 'dp', 'mp')
- exit_mean: float32 [2], replicated
Inputs may be any that keep to these rules, and one draw needn't show every extreme that they name: `layer_mask`: every layer is run by at least one micro-batch.
All inputs are finite; a program needn't handle non-finite values.
Results may differ from a plain program's by a relative error of at most 0.0003.
Values sent between devices are 32-bit elements; how exact they have to be, the bound alone decides.
A program may use at most 64 MiB of HBM per device.

v0:
```python
import jax
import jax.numpy as jnp
from jax import lax
from jax.experimental import pallas as pl
from jax.experimental.pallas import tpu as pltpu
from jax.sharding import PartitionSpec as P

max_rms = 1.0
eps_norm = 1e-06
eps_adam = 1e-08
beta_one = 0.9
beta_two = 0.95
learn_rate = 0.01
decay_rate = 0.1

MESH_ID = pl.DeviceIdType.MESH
ROWS = 256
LANES = 128
LAG = 1
MINE, OTHER = 0, 1


def update(gradient, clip_scale, params, moment, second):
    clipped = clip_scale * gradient
    new_moment = beta_one * moment + (1.0 - beta_one) * clipped
    new_second = beta_two * second + (1.0 - beta_two) * clipped * clipped
    new_params = params - learn_rate * (
        new_moment / (jnp.sqrt(new_second) + eps_adam) + decay_rate * params
    )
    return new_params, new_moment, new_second


def any_mesh_body(entries, gradients, layer_mask, exit_losses, exit_weights, params, moment, second):
    keep_float = layer_mask[0].astype(jnp.float32)
    loss_terms = keep_float * exit_losses[0]
    local_term = gradients[0].astype(jnp.float32) * keep_float[:, None, None]
    summed = lax.psum_scatter(local_term, "dp", scatter_dimension=1, tiled=True)
    weight_float = exit_weights.astype(jnp.float32)
    weight_sum = jnp.sum(weight_float)
    layer_count, loss_sum = lax.psum((keep_float, loss_terms), "dp")
    gradient = summed * (weight_float / (weight_sum * layer_count))[:, None, None]
    square_sum = lax.psum(jnp.sum(gradient * gradient), ("dp", "mp"))
    rms_value = jnp.sqrt(square_sum / entries)
    clip_scale = jnp.minimum(1.0, max_rms / (rms_value + eps_norm))
    new = update(gradient, clip_scale, params, moment, second)
    return (*new, loss_sum / layer_count)


def line_kernel(
    n_mp, entries, mask_in, losses_in, weights_in, grads, out, stats_out, clip_out,
    mask, losses, weights, held, snd, xr, zr, ar, st0, st1, square,
    small_sem, load_sem, send_sem, x_sem, z_sem, a_sem,
    st0_send, st0_recv, st1_send, st1_recv,
):
    layers, rows = out.shape[0], out.shape[1]
    pieces = snd.shape[1]
    depth = snd.shape[2]
    per_layer = pieces // layers
    early = pieces // 2
    dp, mp = lax.axis_index("dp"), lax.axis_index("mp")
    z, x = dp // 2, lax.rem(dp, 2)
    upper = z // 2
    place = lax.rem(z + upper, 2)
    x_dev = z * 2 + 1 - x
    z_dev = (z + 1 - 2 * lax.rem(z, 2)) * 2 + x
    a_dev = (3 - z) * 2 + x

    barrier = pltpu.get_barrier_semaphore()
    devices = 8 * n_mp
    place_in_all = dp * n_mp + mp

    def away(i):
        peer = lax.rem(place_in_all + i, devices)
        return peer, {"dp": peer // n_mp, "mp": lax.rem(peer, n_mp)}

    for i in range(1, devices):
        pl.semaphore_signal(barrier, inc=1, device_id=away(i)[1], device_id_type=MESH_ID)

    small = [
        pltpu.make_async_copy(src, dst, small_sem.at[i])
        for i, (src, dst) in enumerate(((mask_in, mask), (losses_in, losses), (weights_in, weights)))
    ]
    for copy in small:
        copy.start()

    def load(slot, layer):
        k, side = slot // 2, slot % 2
        target = (k + upper * (3 - 2 * k)) * 2 + (x if side == MINE else 1 - x)
        return pltpu.make_async_copy(
            grads.at[0, layer, pl.ds(target * rows, rows), :], held.at[slot, layer], load_sem.at[slot, layer]
        )

    order = (7, 3, 1, 6, 5, 4, 2, 0)
    for slot in order:
        for layer in range(layers):
            load(slot, layer).start()

    def loaded(*slots):
        for slot in slots:
            for layer in range(layers):
                load(slot, layer).wait()

    for copy in small:
        copy.wait()
    lane = lax.broadcasted_iota(jnp.int32, st0.shape[1:], 1)
    tile = jnp.zeros(st0.shape[1:], jnp.float32)
    for layer in range(layers):
        keep = mask[0, layer].astype(jnp.float32)
        tile = jnp.where(lane == layer, keep, tile)
        tile = jnp.where(lane == layers + layer, keep * losses[0, layer], tile)
    st0[dp] = tile

    pl.semaphore_wait(barrier, devices - 1)

    def own(slot, c):
        layer, r = c // per_layer, lax.rem(c, per_layer)
        keep = mask[0, layer].astype(jnp.float32)
        return held[slot, layer, pl.ds(pl.multiple_of(r * depth, depth), depth), :].astype(jnp.float32) * keep

    def push(slot, c, dst, sem, device):
        return pltpu.make_async_remote_copy(
            src_ref=snd.at[slot, c], dst_ref=dst, send_sem=send_sem.at[slot, c], recv_sem=sem,
            device_id={"dp": device}, device_id_type=MESH_ID,
        )

    def to_x(k, c):
        return push(2 * k + OTHER, c, xr.at[k, c], x_sem.at[k, c], x_dev)

    def to_z(slot, box, c):
        return push(slot, c, zr.at[box, c], z_sem.at[box, c], z_dev)

    def to_a(k, c):
        return push(2 * k + MINE, c, ar.at[3 - k, c], a_sem.at[3 - k, c], a_dev)

    def from_x(k, c):
        to_x(k, c).wait_recv()
        return xr[k, c]

    def from_z(box, c):
        to_z(0, box, c).wait_recv()
        return zr[box, c]

    def from_a(box, c):
        to_a(3 - box, c).wait_recv()
        return ar[box, c]

    def each(low, high, step):
        def one(c, carry):
            step(c)
            return carry

        lax.fori_loop(low, high, one, 0)

    def x_own(k, c):
        snd[2 * k + OTHER, c] = own(2 * k + OTHER, c)
        to_x(k, c).start()

    def share_stats(i):
        return pltpu.make_async_remote_copy(
            src_ref=st0.at[dp], dst_ref=st0.at[dp], send_sem=st0_send.at[i], recv_sem=st0_recv.at[dp],
            device_id={"dp": lax.rem(dp + i, 8)}, device_id_type=MESH_ID,
        )

    def stats_arrival(i):
        peer = lax.rem(dp + i, 8)
        return pltpu.make_async_remote_copy(
            src_ref=st0.at[dp], dst_ref=st0.at[peer], send_sem=st0_send.at[i], recv_sem=st0_recv.at[peer],
            device_id={"dp": peer}, device_id_type=MESH_ID,
        )

    @pl.when(place == 0)
    def _():
        loaded(7, 3)

        def first(c):
            x_own(3, c)

            @pl.when(c < early)
            def _():
                snd[3, c] = own(3, c)
                to_z(3, 0, c).start()

        each(0, pieces, first)
        loaded(1, 6, 5)
        for i in range(1, 8):
            share_stats(i).start()

        def second(c):
            snd[6, c] = own(6, c) + from_x(3, c)
            to_z(6, 3, c).start()
            x_own(2, c)

        each(0, pieces, second)
        loaded(4, 2, 0)

        def send_own_level(c):
            snd[1, c] = own(1, c) + from_z(1, c)
            to_x(0, c).start()

        def third(c):
            snd[4, c] = own(4, c) + from_x(2, c)
            to_z(4, 2, c).start()

        def third_a(c):
            third(c)
            x_own(1, c + early)

        def third_b(c):
            third(c)
            send_own_level(c - (pieces - early))

        each(0, pieces - early, third_a)
        each(pieces - early, pieces, third_b)

        def fourth(c):
            snd[2, c] = own(2, c) + from_x(1, c)
            to_z(2, 1, c).start()
            send_own_level(c)

        each(early, pieces, fourth)

        def fifth(c):
            snd[2, c] = own(2, c)
            to_z(2, 1, c).start()

        each(0, early, fifth)

    @pl.when(place == 1)
    def _():
        loaded(7, 1)

        def first(c):
            x_own(3, c)
            snd[1, c] = own(1, c)
            to_z(1, 1, c).start()

        each(0, pieces, first)
        loaded(3, 6, 5)
        for i in range(1, 8):
            share_stats(i).start()
        loaded(4, 2, 0)

        def pass_out(c):
            snd[0, c] = own(0, c) + from_a(0, c)
            to_z(0, 0, c).start()

        def second(c):
            x_own(2, c)
            snd[6, c] = own(6, c) + from_x(3, c) + from_z(3, c)
            to_a(3, c).start()

        def second_b(c):
            second(c)
            pass_out(c - LAG)

        each(0, LAG, second)
        each(LAG, pieces, second_b)

        def third(c):
            snd[4, c] = own(4, c) + from_x(2, c) + from_z(2, c)
            to_a(2, c).start()

        def third_a(c):
            x_own(1, c + early)
            third(c)

            @pl.when(c < LAG)
            def _():
                pass_out(c + pieces - LAG)

        def third_b(c):
            late = c - (pieces - early)
            snd[3, late] = own(3, late) + from_z(0, late)
            to_x(1, late).start()
            third(c)

        each(0, pieces - early, third_a)
        each(pieces - early, pieces, third_b)

    for i in range(1, 8):
        stats_arrival(i).wait_recv()
    total = st0[0]
    for i in range(1, 8):
        total = total + st0[i]
    stats_out[...] = total
    weight_sum = weights[0].astype(jnp.float32)
    for layer in range(1, layers):
        weight_sum = weight_sum + weights[layer].astype(jnp.float32)
    square[...] = jnp.zeros_like(square)
    factors = [weights[layer].astype(jnp.float32) / (weight_sum * total[:, layer : layer + 1]) for layer in range(layers)]

    def finish(layer, c, summed):
        factor = factors[layer]
        gradient = summed * factor
        r = lax.rem(c, per_layer)
        out[layer, pl.ds(pl.multiple_of(r * depth, depth), depth), :] = gradient
        squares = gradient * gradient
        square[...] += jnp.sum(squares.reshape(depth // 8, 8, squares.shape[1]), axis=0)

    @pl.when(place == 0)
    def _():
        for layer in range(layers):
            def last(c, layer=layer):
                finish(layer, c, own(0, c) + from_z(0, c) + from_x(0, c))

            each(layer * per_layer, (layer + 1) * per_layer, last)

    @pl.when(place == 1)
    def _():
        for layer in list(range(layers))[::-1]:
            def last(c, layer=layer):
                finish(layer, c, own(2, c) + from_x(1, c) + from_a(1, c) + from_z(1, c))

            each(layer * per_layer, (layer + 1) * per_layer, last)

    def share_square(i):
        return pltpu.make_async_remote_copy(
            src_ref=st1.at[place_in_all], dst_ref=st1.at[place_in_all],
            send_sem=st1_send.at[i], recv_sem=st1_recv.at[place_in_all],
            device_id=away(i)[1], device_id_type=MESH_ID,
        )

    def square_arrival(i):
        peer, device = away(i)
        return pltpu.make_async_remote_copy(
            src_ref=st1.at[place_in_all], dst_ref=st1.at[peer], send_sem=st1_send.at[i], recv_sem=st1_recv.at[peer],
            device_id=device, device_id_type=MESH_ID,
        )

    folded = jnp.sum(square[...], axis=0, keepdims=True)
    st1[place_in_all] = sum(folded[:, i : i + LANES] for i in range(0, folded.shape[1], LANES))
    for i in range(1, devices):
        share_square(i).start()
    for i in range(1, devices):
        square_arrival(i).wait_recv()
    all_rows = st1[0]
    for i in range(1, devices):
        all_rows = all_rows + st1[i]
    square_sum = jnp.sum(all_rows, keepdims=True)
    rms_value = jnp.sqrt(square_sum / entries)
    clip_out[...] = jnp.broadcast_to(jnp.minimum(1.0, max_rms / (rms_value + eps_norm)), clip_out.shape)

    for i in range(1, 8):
        share_stats(i).wait_send()
    for i in range(1, devices):
        share_square(i).wait_send()

    def sent(slot):
        each(0, pieces, lambda c: to_z(slot, 0, c).wait_send())

    for slot in range(1, 8):
        if slot != 2:
            sent(slot)

    @pl.when(place == 0)
    def _():
        sent(2)

    @pl.when(place == 1)
    def _():
        sent(0)


def line_body(n_mp, entries, gradients, layer_mask, exit_losses, exit_weights, params, moment, second):
    layers, rows, columns = params.shape
    depth = min(ROWS, rows)
    pieces = layers * (rows // depth)
    vmem = pl.BlockSpec(memory_space=pltpu.VMEM)
    block = (pieces, depth, columns)
    f32, dma = jnp.float32, pltpu.SemaphoreType.DMA
    tile = (8, columns)

    def kernel(*refs):
        line_kernel(n_mp, entries, *refs)

    gradient, stats, clip = pl.pallas_call(
        kernel,
        name="line_reduce",
        out_shape=(
            jax.ShapeDtypeStruct((layers, rows, columns), f32),
            jax.ShapeDtypeStruct((1, LANES), f32),
            jax.ShapeDtypeStruct((1, columns), f32),
        ),
        in_specs=[pl.BlockSpec(memory_space=pltpu.HBM)] * 4,
        out_specs=(vmem, vmem, vmem),
        scratch_shapes=[
            pltpu.SMEM(layer_mask.shape, layer_mask.dtype),
            pltpu.SMEM(exit_losses.shape, exit_losses.dtype),
            pltpu.SMEM(exit_weights.shape, exit_weights.dtype),
            pltpu.VMEM((8, layers, rows, columns), gradients.dtype),
            pltpu.VMEM((8, *block), f32),
            pltpu.VMEM((4, *block), f32),
            pltpu.VMEM((4, *block), f32),
            pltpu.VMEM((2, *block), f32),
            pltpu.VMEM((8, 1, LANES), f32),
            pltpu.VMEM((8 * n_mp, 1, LANES), f32),
            pltpu.VMEM(tile, f32),
            dma((3,)), dma((8, layers)), dma((8, pieces)), dma((4, pieces)), dma((4, pieces)), dma((2, pieces)),
            dma((8,)), dma((8,)), dma((8 * n_mp,)), dma((8 * n_mp,)),
        ],
        compiler_params=pltpu.CompilerParams(
            collective_id=0, has_side_effects=True, vmem_limit_bytes=32 * 1024 * 1024
        ),
    )(*(pltpu.with_memory_space_constraint(a, pltpu.HBM) for a in (layer_mask, exit_losses, exit_weights, gradients)))
    exit_mean = stats[0, layers : 2 * layers] / stats[0, :layers]
    new = update(gradient, clip[None], params, moment, second)
    return (*new, exit_mean)


def solution(mesh):
    state = P(None, "dp", "mp")
    placed = (P("dp", None, None, "mp"), P("dp", None), P("dp", None), P(), state, state, state)
    n_dp, n_mp = mesh.shape["dp"], mesh.shape["mp"]

    def whole(*args):
        entries = args[4].size
        layers = args[4].shape[0]

        def body(*blocks):
            if n_dp == 8 and layers == 2:
                return line_body(n_mp, entries, *blocks)
            return any_mesh_body(entries, *blocks)

        return jax.shard_map(
            body, mesh=mesh, in_specs=placed, out_specs=(state, state, state, P()), check_vma=False
        )(*args)

    return whole
```

profile of v0, /device:TPU:0, one launch (start us, length us, event | category | flops | bytes accessed | tf_op | source)
XLA Modules:
  0.0 96.2 jit_solution(8256859738149257854)
XLA Ops:
  0.6 0.0 copy-start.1
  0.6 0.0 copy-start.2
  0.7 0.0 copy-start
  0.7 92.8 %line_reduce.1 = (f32[2,512,256]{2,1,0:T(8,128)S(1)}, f32[1,128]{1,0:T(1,128)S(1)}, f32[1,256]{1,0:T(1,128)S(1)}) custom-call(s32[1,2]{1,0:T(1,128)} %refs_0_.1, f32[1,2]{1,0:T(1,128)} %refs_1_.1, s32[2]{0:T(128)} %refs_2_.1, bf16[1,2,4096,256]{3,2,1,0:T(8,128)(2,1)} %refs_3_.1), custom_call_target="tpu_custom_call" | custom-call | tf_op jit(solution)/shard_map/line_reduce/pallas_call | solution.py:376
  93.5 0.6 fusion.1
  94.1 0.0 copy-done.1
  94.1 0.0 copy-done.2
  94.1 0.0 copy-done
  94.1 2.2 %multiply_subtract_fusion = (f32[2,512,256]{2,1,0:T(8,128)}, f32[2,512,256]{2,1,0:T(8,128)}, f32[2,512,256]{2,1,0:T(8,128)}) fusion(f32[2,512,256]{2,1,0:T(8,128)S(1)} %copy-done, f32[2,512,256]{2,1,0:T(8,128)S(1)} %get-tuple-element.8, f32[256]{0:T(256)S(1)} %bitcast.3, f32[2,512,256]{2,1,0:T(8,128)S(1)} %copy-done.1, f32[2,512,256]{2,1,0:T(8,128)S(1)} %copy-done.2), kind=kLoop, calls=%fused_computation.2 | loop fusion | flops 3670016 | bytes 7341056 | tf_op jit(solution)/shard_map/sub | solution.py:27
Async XLA Ops:
  0.6 93.4 %copy-start.1 = (f32[2,512,256]{2,1,0:T(8,128)S(1)}, f32[2,512,256]{2,1,0:T(8,128)}, u32[]{:S(2)}) copy-start(f32[2,512,256]{2,1,0:T(8,128)} %param.13) | copy-start | bytes 3145732
  0.6 93.4 %copy-start.2 = (f32[2,512,256]{2,1,0:T(8,128)S(1)}, f32[2,512,256]{2,1,0:T(8,128)}, u32[]{:S(2)}) copy-start(f32[2,512,256]{2,1,0:T(8,128)} %param.12) | copy-start | bytes 3145732
  0.7 93.4 %copy-start = (f32[2,512,256]{2,1,0:T(8,128)S(1)}, f32[2,512,256]{2,1,0:T(8,128)}, u32[]{:S(2)}) copy-start(f32[2,512,256]{2,1,0:T(8,128)} %param.11) | copy-start | bytes 3145732
where the time goes:
time: 96.4 us; the launch traced here: 96.2 us
  Pallas kernels  92.8 us (96%)
  other arithmetic  2.75 us (3%)
    pallas_call x1, Pallas kernels, line_body(): pl.pallas_call(kernel, name='line_reduce', out_shape=(jax.ShapeDtypeStruc...  92.8 us
    sub x1, other arithmetic, update(): params - learn_rate * (new_moment / (jnp.sqrt(new_second) + eps_adam) + d...  2.16 us

commit v1 on v0

--- a/solution.py
+++ b/solution.py
@@ -14,9 +14,10 @@
 decay_rate = 0.1
 
 MESH_ID = pl.DeviceIdType.MESH
-ROWS = 256
+ROWS = 64
 LANES = 128
-LAG = 1
+LAG = 4
+CHUNKS = 8
 MINE, OTHER = 0, 1
 
 
@@ -47,10 +48,11 @@
 
 
 def line_kernel(
-    n_mp, entries, mask_in, losses_in, weights_in, grads, out, stats_out, clip_out,
+    n_mp, entries, mask_in, losses_in, weights_in, grads, params_in, moment_in, second_in,
+    out, params_out, moment_out, second_out, stats_out, clip_out,
     mask, losses, weights, held, snd, xr, zr, ar, st0, st1, square,
-    small_sem, load_sem, send_sem, x_sem, z_sem, a_sem,
-    st0_send, st0_recv, st1_send, st1_recv,
+    small_sem, load_sem, state_sem, send_sem, x_sem, z_sem, a_sem,
+    st0_send, st0_recv, st1_send, st1_recv, y_in, x_in, end_in, middle_in, all_in,
 ):
     layers, rows = out.shape[0], out.shape[1]
     pieces = snd.shape[1]
@@ -70,11 +72,19 @@
     place_in_all = dp * n_mp + mp
 
     def away(i):
-        peer = lax.rem(place_in_all + i, devices)
-        return peer, {"dp": peer // n_mp, "mp": lax.rem(peer, n_mp)}
-
-    for i in range(1, devices):
-        pl.semaphore_signal(barrier, inc=1, device_id=away(i)[1], device_id_type=MESH_ID)
+        other_z, other_x, other_mp = z ^ (i // (2 * n_mp)), x ^ (i // n_mp % 2), mp ^ (i % n_mp)
+        other_dp = other_z * 2 + other_x
+        return other_dp * n_mp + other_mp, {"dp": other_dp, "mp": other_mp}
+
+    def greet(sem, device):
+        pl.semaphore_signal(sem, inc=1, device_id=device, device_id_type=MESH_ID)
+
+    for device in ({"dp": x_dev}, {"dp": z_dev}, {"mp": mp ^ 1}, {"mp": mp ^ 2}):
+        greet(barrier, device)
+
+    @pl.when(place == 1)
+    def _():
+        greet(barrier, {"dp": a_dev})
 
     small = [
         pltpu.make_async_copy(src, dst, small_sem.at[i])
@@ -90,10 +100,18 @@
             grads.at[0, layer, pl.ds(target * rows, rows), :], held.at[slot, layer], load_sem.at[slot, layer]
         )
 
-    order = (7, 3, 1, 6, 5, 4, 2, 0)
-    for slot in order:
-        for layer in range(layers):
-            load(slot, layer).start()
+    def fetch(*slots):
+        for slot in slots:
+            for layer in range(layers):
+                load(slot, layer).start()
+
+    def state():
+        pairs = ((params_in, params_out), (moment_in, moment_out), (second_in, second_out))
+        return [pltpu.make_async_copy(src, dst, state_sem.at[i]) for i, (src, dst) in enumerate(pairs)]
+
+    fetch(7)
+    pl.when(place == 0)(lambda: fetch(3))
+    pl.when(place == 1)(lambda: fetch(1))
 
     def loaded(*slots):
         for slot in slots:
@@ -110,7 +128,26 @@
         tile = jnp.where(lane == layers + layer, keep * losses[0, layer], tile)
     st0[dp] = tile
 
-    pl.semaphore_wait(barrier, devices - 1)
+    pl.when(place == 0)(lambda: pl.semaphore_wait(barrier, 4))
+    pl.when(place == 1)(lambda: pl.semaphore_wait(barrier, 5))
+
+    def meet():
+        greet(y_in, {"mp": mp ^ 2})
+        pl.semaphore_wait(y_in, 1)
+        greet(x_in, {"dp": x_dev})
+        pl.semaphore_wait(x_in, 1)
+
+        @pl.when(place == 0)
+        def _():
+            greet(end_in, {"dp": z_dev})
+            pl.semaphore_wait(all_in, 1)
+
+        @pl.when(place == 1)
+        def _():
+            pl.semaphore_wait(end_in, 1)
+            greet(middle_in, {"dp": a_dev})
+            pl.semaphore_wait(middle_in, 1)
+            greet(all_in, {"dp": z_dev})
 
     def own(slot, c):
         layer, r = c // per_layer, lax.rem(c, per_layer)
@@ -119,7 +156,7 @@
 
     def push(slot, c, dst, sem, device):
         return pltpu.make_async_remote_copy(
-            src_ref=snd.at[slot, c], dst_ref=dst, send_sem=send_sem.at[slot, c], recv_sem=sem,
+            src_ref=snd.at[slot, c], dst_ref=dst, send_sem=send_sem.at[slot], recv_sem=sem,
             device_id={"dp": device}, device_id_type=MESH_ID,
         )
 
@@ -180,7 +217,12 @@
                 snd[3, c] = own(3, c)
                 to_z(3, 0, c).start()
 
-        each(0, pieces, first)
+        each(0, 1, first)
+        fetch(6, 5, 1, 4, 2, 0)
+        each(1, pieces, first)
+        meet()
+        for copy in state():
+            copy.start()
         loaded(1, 6, 5)
         for i in range(1, 8):
             share_stats(i).start()
@@ -234,7 +276,12 @@
             snd[1, c] = own(1, c)
             to_z(1, 1, c).start()
 
-        each(0, pieces, first)
+        each(0, 1, first)
+        fetch(6, 5, 3, 4, 2, 0)
+        each(1, pieces, first)
+        meet()
+        for copy in state():
+            copy.start()
         loaded(3, 6, 5)
         for i in range(1, 8):
             share_stats(i).start()
@@ -327,9 +374,11 @@
             device_id=device, device_id_type=MESH_ID,
         )
 
+    for copy in state():
+        copy.wait()
     folded = jnp.sum(square[...], axis=0, keepdims=True)
     st1[place_in_all] = sum(folded[:, i : i + LANES] for i in range(0, folded.shape[1], LANES))
-    for i in range(1, devices):
+    for i in range(devices - 1, 0, -1):
         share_square(i).start()
     for i in range(1, devices):
         square_arrival(i).wait_recv()
@@ -346,43 +395,64 @@
         share_square(i).wait_send()
 
     def sent(slot):
-        each(0, pieces, lambda c: to_z(slot, 0, c).wait_send())
+        pltpu.make_async_remote_copy(
+            src_ref=snd.at[slot], dst_ref=zr.at[0], send_sem=send_sem.at[slot], recv_sem=z_sem.at[0, 0],
+            device_id={"dp": z_dev}, device_id_type=MESH_ID,
+        ).wait_send()
 
     for slot in range(1, 8):
         if slot != 2:
             sent(slot)
 
-    @pl.when(place == 0)
-    def _():
-        sent(2)
-
-    @pl.when(place == 1)
-    def _():
-        sent(0)
+    pl.when(place == 0)(lambda: sent(2))
+    pl.when(place == 1)(lambda: sent(0))
+
+
+def update_kernel(gradient, params, moment, second, stats, clip, params_out, moment_out, second_out, mean_out, news, sem):
+    layers, rows = gradient.shape[0], gradient.shape[1]
+    outs = (params_out, moment_out, second_out)
+    depth = rows * layers // CHUNKS
+    per_layer = rows // depth
+
+    def put(i, layer, part):
+        window = (layer, pl.ds(part * depth, depth))
+        return pltpu.make_async_copy(news.at[(i, *window)], outs[i].at[window], sem.at[i, layer, part])
+
+    chunks = [(layer, part) for layer in range(layers) for part in range(per_layer)]
+    for layer, part in chunks:
+        window = (layer, pl.ds(part * depth, depth))
+        new = update(gradient[window], clip[...], params[window], moment[window], second[window])
+        for i in range(3):
+            news[(i, *window)] = new[i]
+            put(i, layer, part).start()
+    mean_out[...] = stats[:, layers : 2 * layers] / stats[:, :layers]
+    for layer, part in chunks:
+        for i in range(3):
+            put(i, layer, part).wait()
 
 
 def line_body(n_mp, entries, gradients, layer_mask, exit_losses, exit_weights, params, moment, second):
     layers, rows, columns = params.shape
     depth = min(ROWS, rows)
     pieces = layers * (rows // depth)
-    vmem = pl.BlockSpec(memory_space=pltpu.VMEM)
+    vmem, hbm = pl.BlockSpec(memory_space=pltpu.VMEM), pl.BlockSpec(memory_space=pltpu.HBM)
     block = (pieces, depth, columns)
-    f32, dma = jnp.float32, pltpu.SemaphoreType.DMA
-    tile = (8, columns)
+    f32, dma, regular = jnp.float32, pltpu.SemaphoreType.DMA, pltpu.SemaphoreType.REGULAR
+    state = jax.ShapeDtypeStruct((layers, rows, columns), f32)
 
     def kernel(*refs):
         line_kernel(n_mp, entries, *refs)
 
-    gradient, stats, clip = pl.pallas_call(
+    *held, stats, clip = pl.pallas_call(
         kernel,
         name="line_reduce",
         out_shape=(
-            jax.ShapeDtypeStruct((layers, rows, columns), f32),
+            state, state, state, state,
             jax.ShapeDtypeStruct((1, LANES), f32),
             jax.ShapeDtypeStruct((1, columns), f32),
         ),
-        in_specs=[pl.BlockSpec(memory_space=pltpu.HBM)] * 4,
-        out_specs=(vmem, vmem, vmem),
+        in_specs=[hbm] * 7,
+        out_specs=[vmem] * 6,
         scratch_shapes=[
             pltpu.SMEM(layer_mask.shape, layer_mask.dtype),
             pltpu.SMEM(exit_losses.shape, exit_losses.dtype),
@@ -394,17 +464,27 @@
             pltpu.VMEM((2, *block), f32),
             pltpu.VMEM((8, 1, LANES), f32),
             pltpu.VMEM((8 * n_mp, 1, LANES), f32),
-            pltpu.VMEM(tile, f32),
-            dma((3,)), dma((8, layers)), dma((8, pieces)), dma((4, pieces)), dma((4, pieces)), dma((2, pieces)),
-            dma((8,)), dma((8,)), dma((8 * n_mp,)), dma((8 * n_mp,)),
+            pltpu.VMEM((8, columns), f32),
+            dma((3,)), dma((8, layers)), dma((3,)), dma((8,)), dma((4, pieces)), dma((4, pieces)), dma((2, pieces)),
+            dma((8,)), dma((8,)), dma((8 * n_mp,)), dma((8 * n_mp,)), regular, regular, regular, regular, regular,
         ],
         compiler_params=pltpu.CompilerParams(
-            collective_id=0, has_side_effects=True, vmem_limit_bytes=32 * 1024 * 1024
+            collective_id=0, has_side_effects=True, vmem_limit_bytes=40 * 1024 * 1024
         ),
-    )(*(pltpu.with_memory_space_constraint(a, pltpu.HBM) for a in (layer_mask, exit_losses, exit_weights, gradients)))
-    exit_mean = stats[0, layers : 2 * layers] / stats[0, :layers]
-    new = update(gradient, clip[None], params, moment, second)
-    return (*new, exit_mean)
+    )(*(
+        pltpu.with_memory_space_constraint(a, pltpu.HBM)
+        for a in (layer_mask, exit_losses, exit_weights, gradients, params, moment, second)
+    ))
+    *new, mean = pl.pallas_call(
+        update_kernel,
+        name="update",
+        out_shape=(state, state, state, jax.ShapeDtypeStruct((1, layers), f32)),
+        in_specs=[vmem] * 6,
+        out_specs=(hbm, hbm, hbm, vmem),
+        scratch_shapes=[pltpu.VMEM((3, layers, rows, columns), f32), dma((3, layers, CHUNKS // layers))],
+        compiler_params=pltpu.CompilerParams(vmem_limit_bytes=16 * 1024 * 1024),
+    )(*held, stats, clip)
+    return (*new, mean[0])
 
 
 def solution(mesh):
@@ -417,7 +497,7 @@
         layers = args[4].shape[0]
 
         def body(*blocks):
-            if n_dp == 8 and layers == 2:
+            if n_dp == 8 and n_mp == 4 and layers == 2:
                 return line_body(n_mp, entries, *blocks)
             return any_mesh_body(entries, *blocks)
 

time: 96.4 us -> 95.9 us (level)
  other arithmetic: 2.75 us -> 0 us
  Pallas kernels: 92.8 us -> 95.1 us
    pallas_call x1 -> x2, Pallas kernels: 92.8 us -> 95.1 us  [the longest x1 92.6 us: line_body(): pl.pallas_call(kernel, name='line_reduce', out_shape=(state, state, state...]
    sub x1 -> x0, other arithmetic: 2.16 us -> none  [update(): params - learn_rate * (new_moment / (jnp.sqrt(new_second) + eps_adam) + d...]
where the time goes in v1:
time: 95.9 us; the launch traced here: 95.8 us
  Pallas kernels  95.1 us (99%)
    pallas_call x1, Pallas kernels, line_body(): pl.pallas_call(kernel, name='line_reduce', out_shape=(state, state, state...  92.6 us
    pallas_call x1, Pallas kernels, line_body(): pl.pallas_call(update_kernel, name='update', out_shape=(state, state, sta...  2.53 us

profile of v1, /device:TPU:0, one launch (start us, length us, event | category | flops | bytes accessed | tf_op | source)
XLA Modules:
  0.0 95.8 jit_solution(12408317486883676693)
XLA Ops:
  0.6 92.6 %line_reduce.1 = (f32[2,512,256]{2,1,0:T(8,128)S(1)}, f32[2,512,256]{2,1,0:T(8,128)S(1)}, f32[2,512,256]{2,1,0:T(8,128)S(1)}, f32[2,512,256]{2,1,0:T(8,128)S(1)}...) custom-call(s32[1,2]{1,0:T(1,128)} %refs_0_.1, f32[1,2]{1,0:T(1,128)} %refs_1_.1, s32[2]{0:T(128)} %refs_2_.1, ...), custom_call_target="tpu_custom_call" | custom-call | tf_op jit(solution)/shard_map/line_reduce/pallas_call | solution.py:446
  93.3 2.5 %update.1 = (f32[2,512,256]{2,1,0:T(8,128)}, f32[2,512,256]{2,1,0:T(8,128)}, f32[2,512,256]{2,1,0:T(8,128)}, f32[1,2]{1,0:T(1,128)}) custom-call(f32[2,512,256]{2,1,0:T(8,128)S(1)} %get-tuple-element.14.gradient, f32[2,512,256]{2,1,0:T(8,128)S(1)} %get-tuple-element.15.params, f32[2,512,256]{2,1,0:T(8,128)S(1)} %get-tuple-element.16.moment, ...), custom_call_target="tpu_custom_call" | custom-call | tf_op jit(solution)/shard_map/update/pallas_call | solution.py:478

commit v2 on v1

--- a/solution.py
+++ b/solution.py
@@ -17,7 +17,12 @@
 ROWS = 64
 LANES = 128
 LAG = 4
-CHUNKS = 8
+EARLY = 10
+TAIL = 6
+START = 11
+PACED = 4
+CHUNK = 256
+STEP = 32
 MINE, OTHER = 0, 1
 
 
@@ -50,15 +55,22 @@
 def line_kernel(
     n_mp, entries, mask_in, losses_in, weights_in, grads, params_in, moment_in, second_in,
     out, params_out, moment_out, second_out, stats_out, clip_out,
-    mask, losses, weights, held, snd, xr, zr, ar, st0, st1, square,
-    small_sem, load_sem, state_sem, send_sem, x_sem, z_sem, a_sem,
+    mask, losses, weights, held, snd, xr, zr, ar, tr, st0, st1, square,
+    small_sem, load_sem, state_sem, send_sem, x_sem, z_sem, a_sem, t_sem,
     st0_send, st0_recv, st1_send, st1_recv, y_in, x_in, end_in, middle_in, all_in,
 ):
     layers, rows = out.shape[0], out.shape[1]
     pieces = snd.shape[1]
     depth = snd.shape[2]
     per_layer = pieces // layers
-    early = pieces // 2
+    early, tail = EARLY, EARLY - TAIL
+    small = [
+        pltpu.make_async_copy(src, dst, small_sem.at[i])
+        for i, (src, dst) in enumerate(((mask_in, mask), (losses_in, losses), (weights_in, weights)))
+    ]
+    for copy in small:
+        copy.start()
+
     dp, mp = lax.axis_index("dp"), lax.axis_index("mp")
     z, x = dp // 2, lax.rem(dp, 2)
     upper = z // 2
@@ -79,20 +91,6 @@
     def greet(sem, device):
         pl.semaphore_signal(sem, inc=1, device_id=device, device_id_type=MESH_ID)
 
-    for device in ({"dp": x_dev}, {"dp": z_dev}, {"mp": mp ^ 1}, {"mp": mp ^ 2}):
-        greet(barrier, device)
-
-    @pl.when(place == 1)
-    def _():
-        greet(barrier, {"dp": a_dev})
-
-    small = [
-        pltpu.make_async_copy(src, dst, small_sem.at[i])
-        for i, (src, dst) in enumerate(((mask_in, mask), (losses_in, losses), (weights_in, weights)))
-    ]
-    for copy in small:
-        copy.start()
-
     def load(slot, layer):
         k, side = slot // 2, slot % 2
         target = (k + upper * (3 - 2 * k)) * 2 + (x if side == MINE else 1 - x)
@@ -109,7 +107,15 @@
         pairs = ((params_in, params_out), (moment_in, moment_out), (second_in, second_out))
         return [pltpu.make_async_copy(src, dst, state_sem.at[i]) for i, (src, dst) in enumerate(pairs)]
 
-    fetch(7)
+    load(7, 0).start()
+    for device in ({"dp": x_dev}, {"dp": z_dev}, {"mp": mp ^ 1}, {"mp": mp ^ 2}):
+        greet(barrier, device)
+
+    @pl.when(place == 1)
+    def _():
+        greet(barrier, {"dp": a_dev})
+
+    load(7, 1).start()
     pl.when(place == 0)(lambda: fetch(3))
     pl.when(place == 1)(lambda: fetch(1))
 
@@ -169,6 +175,13 @@
     def to_a(k, c):
         return push(2 * k + MINE, c, ar.at[3 - k, c], a_sem.at[3 - k, c], a_dev)
 
+    def to_tail(c):
+        return push(2, c, tr.at[c - tail], t_sem.at[c - tail], z_dev)
+
+    def from_tail(c):
+        to_tail(c).wait_recv()
+        return tr[c - tail]
+
     def from_x(k, c):
         to_x(k, c).wait_recv()
         return xr[k, c]
@@ -207,10 +220,15 @@
 
     @pl.when(place == 0)
     def _():
-        loaded(7, 3)
+        load(7, 0).wait()
+        x_own(3, 0)
+        load(7, 1).wait()
+        loaded(3)
 
         def first(c):
-            x_own(3, c)
+            @pl.when(c > 0)
+            def _():
+                x_own(3, c)
 
             @pl.when(c < early)
             def _():
@@ -265,14 +283,20 @@
             snd[2, c] = own(2, c)
             to_z(2, 1, c).start()
 
-        each(0, early, fifth)
+        each(0, tail, fifth)
 
     @pl.when(place == 1)
     def _():
-        loaded(7, 1)
+        load(7, 0).wait()
+        x_own(3, 0)
+        load(7, 1).wait()
+        loaded(1)
 
         def first(c):
-            x_own(3, c)
+            @pl.when(c > 0)
+            def _():
+                x_own(3, c)
+
             snd[1, c] = own(1, c)
             to_z(1, 1, c).start()
 
@@ -293,6 +317,12 @@
 
         def second(c):
             x_own(2, c)
+
+            @pl.when(c < early)
+            def _():
+                snd[3, c] = own(3, c) + from_z(0, c)
+                to_x(1, c).start()
+
             snd[6, c] = own(6, c) + from_x(3, c) + from_z(3, c)
             to_a(3, c).start()
 
@@ -304,25 +334,42 @@
         each(LAG, pieces, second_b)
 
         def third(c):
+            @pl.when(c < pieces - early)
+            def _():
+                x_own(1, c + early)
+
             snd[4, c] = own(4, c) + from_x(2, c) + from_z(2, c)
             to_a(2, c).start()
-
-        def third_a(c):
-            x_own(1, c + early)
-            third(c)
 
             @pl.when(c < LAG)
             def _():
                 pass_out(c + pieces - LAG)
 
+        def return_tail(c):
+            snd[2, c] = own(2, c) + from_x(1, c) + from_a(1, c)
+            to_tail(c).start()
+
         def third_b(c):
-            late = c - (pieces - early)
-            snd[3, late] = own(3, late) + from_z(0, late)
-            to_x(1, late).start()
             third(c)
-
-        each(0, pieces - early, third_a)
-        each(pieces - early, pieces, third_b)
+            return_tail(c - LAG)
+
+        each(0, tail + LAG, third)
+        each(tail + LAG, early + LAG, third_b)
+        each(early + LAG, pieces, third)
+
+    for copy in state():
+        copy.wait()
+    def weigh(ref, layer, c, factor):
+        window = (layer, pl.ds(pl.multiple_of(c * depth, depth), depth))
+        ref[window] = ref[window] * factor
+
+    for layer in range(layers):
+        def weigh_all(c, layer=layer):
+            weigh(params_out, layer, c, 1.0 - learn_rate * decay_rate)
+            weigh(moment_out, layer, c, beta_one)
+            weigh(second_out, layer, c, beta_two)
+
+        each(0, per_layer, weigh_all)
 
     for i in range(1, 8):
         stats_arrival(i).wait_recv()
@@ -336,29 +383,52 @@
     square[...] = jnp.zeros_like(square)
     factors = [weights[layer].astype(jnp.float32) / (weight_sum * total[:, layer : layer + 1]) for layer in range(layers)]
 
+    def count(gradient):
+        squares = gradient * gradient
+        square[...] += jnp.sum(squares.reshape(depth // 8, 8, squares.shape[1]), axis=0)
+
     def finish(layer, c, summed):
-        factor = factors[layer]
-        gradient = summed * factor
+        gradient = summed * factors[layer]
         r = lax.rem(c, per_layer)
         out[layer, pl.ds(pl.multiple_of(r * depth, depth), depth), :] = gradient
-        squares = gradient * gradient
-        square[...] += jnp.sum(squares.reshape(depth // 8, 8, squares.shape[1]), axis=0)
+        return gradient
+
+    def spans(low, high):
+        cuts = [low, *(b for b in range(per_layer, pieces, per_layer) if low < b < high), high]
+        return [(a // per_layer, a, b) for a, b in zip(cuts, cuts[1:]) if a < b]
+
+    def last(c, layer):
+        return finish(layer, c, own(2, c) + from_x(1, c) + from_a(1, c) + from_z(1, c))
+
+    def finish_only(c, layer):
+        finish(layer, c, snd[2, c] + from_z(1, c))
+
+    def last_end(c, layer):
+        count(finish(layer, c, own(0, c) + from_z(0, c) + from_x(0, c)))
+
+    def count_tail(c, layer):
+        snd[2, c] = own(2, c)
+        count((snd[2, c] + from_tail(c)) * factors[layer])
+
+    def paced(c, layer):
+        to_z(2, 1, c - START + tail).start()
+        last_end(c, layer)
+
+    def over(step, *ranges):
+        for low, high in ranges:
+            for layer, a, b in spans(low, high):
+                each(a, b, lambda c, layer=layer: step(c, layer))
 
     @pl.when(place == 0)
     def _():
-        for layer in range(layers):
-            def last(c, layer=layer):
-                finish(layer, c, own(0, c) + from_z(0, c) + from_x(0, c))
-
-            each(layer * per_layer, (layer + 1) * per_layer, last)
+        over(count_tail, (tail, early))
+        over(last_end, (0, START))
+        over(paced, (START, START + PACED))
+        over(last_end, (START + PACED, pieces))
 
     @pl.when(place == 1)
     def _():
-        for layer in list(range(layers))[::-1]:
-            def last(c, layer=layer):
-                finish(layer, c, own(2, c) + from_x(1, c) + from_a(1, c) + from_z(1, c))
-
-            each(layer * per_layer, (layer + 1) * per_layer, last)
+        over(lambda c, layer: count(last(c, layer)), (early, pieces), (0, tail))
 
     def share_square(i):
         return pltpu.make_async_remote_copy(
@@ -374,12 +444,19 @@
             device_id=device, device_id_type=MESH_ID,
         )
 
-    for copy in state():
-        copy.wait()
     folded = jnp.sum(square[...], axis=0, keepdims=True)
     st1[place_in_all] = sum(folded[:, i : i + LANES] for i in range(0, folded.shape[1], LANES))
     for i in range(devices - 1, 0, -1):
         share_square(i).start()
+
+    @pl.when(place == 0)
+    def _():
+        each(tail + PACED, early, lambda c: to_z(2, 1, c).start())
+
+    @pl.when(place == 1)
+    def _():
+        over(finish_only, (tail, early))
+
     for i in range(1, devices):
         square_arrival(i).wait_recv()
     all_rows = st1[0]
@@ -394,41 +471,57 @@
     for i in range(1, devices):
         share_square(i).wait_send()
 
-    def sent(slot):
+    def sent(slot, low=0, high=pieces):
         pltpu.make_async_remote_copy(
-            src_ref=snd.at[slot], dst_ref=zr.at[0], send_sem=send_sem.at[slot], recv_sem=z_sem.at[0, 0],
+            src_ref=snd.at[slot, pl.ds(low, high - low)], dst_ref=zr.at[0, pl.ds(low, high - low)],
+            send_sem=send_sem.at[slot], recv_sem=z_sem.at[0, 0],
             device_id={"dp": z_dev}, device_id_type=MESH_ID,
         ).wait_send()
 
-    for slot in range(1, 8):
-        if slot != 2:
-            sent(slot)
-
-    pl.when(place == 0)(lambda: sent(2))
-    pl.when(place == 1)(lambda: sent(0))
-
-
-def update_kernel(gradient, params, moment, second, stats, clip, params_out, moment_out, second_out, mean_out, news, sem):
+    for slot in (1, 3, 4, 5, 6, 7):
+        sent(slot)
+
+    @pl.when(place == 0)
+    def _():
+        sent(2)
+
+    @pl.when(place == 1)
+    def _():
+        sent(0)
+        sent(2, tail, early)
+
+
+def update_kernel(gradient, params, moment, second, stats, clip, params_out, moment_out, second_out, mean_out, news, mean, sem, mean_sem):
     layers, rows = gradient.shape[0], gradient.shape[1]
     outs = (params_out, moment_out, second_out)
-    depth = rows * layers // CHUNKS
-    per_layer = rows // depth
-
-    def put(i, layer, part):
-        window = (layer, pl.ds(part * depth, depth))
-        return pltpu.make_async_copy(news.at[(i, *window)], outs[i].at[window], sem.at[i, layer, part])
-
-    chunks = [(layer, part) for layer in range(layers) for part in range(per_layer)]
-    for layer, part in chunks:
-        window = (layer, pl.ds(part * depth, depth))
-        new = update(gradient[window], clip[...], params[window], moment[window], second[window])
+    chunk, step = min(CHUNK, rows), min(STEP, rows)
+    mean[...] = stats[:, layers : 2 * layers] / stats[:, :layers]
+    mean_copy = pltpu.make_async_copy(mean, mean_out, mean_sem)
+    mean_copy.start()
+    clip_scale = clip[...]
+    first_scale = (1.0 - beta_one) * clip_scale
+    second_scale = (1.0 - beta_two) * clip_scale * clip_scale
+
+    def put(i, layer, low):
+        window = (layer, pl.ds(low, chunk))
+        return pltpu.make_async_copy(news.at[(i, *window)], outs[i].at[window], sem.at[i])
+
+    chunks = [(layer, low) for layer in range(layers) for low in range(0, rows, chunk)]
+    for layer, low in chunks:
+        for start in range(low, low + chunk, step):
+            window = (layer, pl.ds(start, step))
+            held = gradient[window]
+            new_moment = moment[window] + first_scale * held
+            new_second = second[window] + second_scale * (held * held)
+            root = new_second * lax.rsqrt(new_second)
+            news[(0, *window)] = params[window] - learn_rate * (new_moment / (root + eps_adam))
+            news[(1, *window)] = new_moment
+            news[(2, *window)] = new_second
         for i in range(3):
-            news[(i, *window)] = new[i]
-            put(i, layer, part).start()
-    mean_out[...] = stats[:, layers : 2 * layers] / stats[:, :layers]
-    for layer, part in chunks:
-        for i in range(3):
-            put(i, layer, part).wait()
+            put(i, layer, low).start()
+    for i in range(3):
+        pltpu.make_async_copy(news.at[i], outs[i], sem.at[i]).wait()
+    mean_copy.wait()
 
 
 def line_body(n_mp, entries, gradients, layer_mask, exit_losses, exit_weights, params, moment, second):
@@ -441,7 +534,10 @@
     state = jax.ShapeDtypeStruct((layers, rows, columns), f32)
 
     def kernel(*refs):
-        line_kernel(n_mp, entries, *refs)
+        pl.run_scoped(lambda *sems: line_kernel(n_mp, entries, *refs, *sems),
+            dma((3,)), dma((8, layers)), dma((3,)), dma((8,)), dma((4, pieces)), dma((4, pieces)), dma((2, pieces)), dma((TAIL,)),
+            dma((8,)), dma((8,)), dma((8 * n_mp,)), dma((8 * n_mp,)), regular, regular, regular, regular, regular,
+        )
 
     *held, stats, clip = pl.pallas_call(
         kernel,
@@ -462,11 +558,10 @@
             pltpu.VMEM((4, *block), f32),
             pltpu.VMEM((4, *block), f32),
             pltpu.VMEM((2, *block), f32),
+            pltpu.VMEM((TAIL, *block[1:]), f32),
             pltpu.VMEM((8, 1, LANES), f32),
             pltpu.VMEM((8 * n_mp, 1, LANES), f32),
             pltpu.VMEM((8, columns), f32),
-            dma((3,)), dma((8, layers)), dma((3,)), dma((8,)), dma((4, pieces)), dma((4, pieces)), dma((2, pieces)),
-            dma((8,)), dma((8,)), dma((8 * n_mp,)), dma((8 * n_mp,)), regular, regular, regular, regular, regular,
         ],
         compiler_params=pltpu.CompilerParams(
             collective_id=0, has_side_effects=True, vmem_limit_bytes=40 * 1024 * 1024
@@ -480,8 +575,8 @@
         name="update",
         out_shape=(state, state, state, jax.ShapeDtypeStruct((1, layers), f32)),
         in_specs=[vmem] * 6,
-        out_specs=(hbm, hbm, hbm, vmem),
-        scratch_shapes=[pltpu.VMEM((3, layers, rows, columns), f32), dma((3, layers, CHUNKS // layers))],
+        out_specs=[hbm] * 4,
+        scratch_shapes=[pltpu.VMEM((3, layers, rows, columns), f32), pltpu.VMEM((1, layers), f32), dma((3,)), dma],
         compiler_params=pltpu.CompilerParams(vmem_limit_bytes=16 * 1024 * 1024),
     )(*held, stats, clip)
     return (*new, mean[0])

time: 95.9 us -> 91.3 us (0.952)
  Pallas kernels: 95.1 us -> 90.5 us
    pallas_call x1, Pallas kernels: 92.6 us -> 88.7 us  [line_body(): pl.pallas_call(kernel, name='line_reduce', out_shape=(state, state, state...]
where the time goes in v2:
time: 91.3 us; the launch traced here: 91.2 us
  Pallas kernels  90.5 us (99%)
    pallas_call x1, Pallas kernels, line_body(): pl.pallas_call(kernel, name='line_reduce', out_shape=(state, state, state...  88.7 us

profile of v2, /device:TPU:0, one launch (start us, length us, event | category | flops | bytes accessed | tf_op | source)
XLA Modules:
  0.0 91.2 jit_solution(18048300167128077407)
XLA Ops:
  0.6 88.7 %line_reduce.1 = (f32[2,512,256]{2,1,0:T(8,128)S(1)}, f32[2,512,256]{2,1,0:T(8,128)S(1)}, f32[2,512,256]{2,1,0:T(8,128)S(1)}, f32[2,512,256]{2,1,0:T(8,128)S(1)}...) custom-call(s32[1,2]{1,0:T(1,128)} %refs_0_.1, f32[1,2]{1,0:T(1,128)} %refs_1_.1, s32[2]{0:T(128)} %refs_2_.1, ...), custom_call_target="tpu_custom_call" | custom-call | tf_op jit(solution)/shard_map/line_reduce/pallas_call | solution.py:542
  89.4 1.8 %update.1 = (f32[2,512,256]{2,1,0:T(8,128)}, f32[2,512,256]{2,1,0:T(8,128)}, f32[2,512,256]{2,1,0:T(8,128)}, f32[1,2]{1,0:T(1,128)}) custom-call(f32[2,512,256]{2,1,0:T(8,128)S(1)} %get-tuple-element.14.gradient, f32[2,512,256]{2,1,0:T(8,128)S(1)} %get-tuple-element.15.params, f32[2,512,256]{2,1,0:T(8,128)S(1)} %get-tuple-element.16.moment, ...), custom_call_target="tpu_custom_call" | custom-call | tf_op jit(solution)/shard_map/update/pallas_call | solution.py:573

commit v3 on v2

--- a/solution.py
+++ b/solution.py
@@ -14,14 +14,14 @@
 decay_rate = 0.1
 
 MESH_ID = pl.DeviceIdType.MESH
-ROWS = 64
+ROWS = 32
 LANES = 128
-LAG = 4
-EARLY = 10
-TAIL = 6
-START = 11
-PACED = 4
-CHUNK = 256
+LAG = 8
+EARLY = (18, 21)
+START = (18, 24)
+PACED = (11, 5)
+TAIL = 13
+CHUNK = 64
 STEP = 32
 MINE, OTHER = 0, 1
 
@@ -55,15 +55,14 @@
 def line_kernel(
     n_mp, entries, mask_in, losses_in, weights_in, grads, params_in, moment_in, second_in,
     out, params_out, moment_out, second_out, stats_out, clip_out,
-    mask, losses, weights, held, snd, xr, zr, ar, tr, st0, st1, square,
+    mask, losses, weights, held, snd, xr, zr, ar, tr, st0, st1, square, factors,
     small_sem, load_sem, state_sem, send_sem, x_sem, z_sem, a_sem, t_sem,
-    st0_send, st0_recv, st1_send, st1_recv, y_in, x_in, end_in, middle_in, all_in,
+    st0_send, st0_recv, st1_send, st1_recv, end_in, core_in, y_in, middle_in, all_in,
 ):
     layers, rows = out.shape[0], out.shape[1]
     pieces = snd.shape[1]
     depth = snd.shape[2]
     per_layer = pieces // layers
-    early, tail = EARLY, EARLY - TAIL
     small = [
         pltpu.make_async_copy(src, dst, small_sem.at[i])
         for i, (src, dst) in enumerate(((mask_in, mask), (losses_in, losses), (weights_in, weights)))
@@ -75,6 +74,12 @@
     z, x = dp // 2, lax.rem(dp, 2)
     upper = z // 2
     place = lax.rem(z + upper, 2)
+
+    def by_half(pair):
+        return pair[0] + upper * (pair[1] - pair[0])
+
+    early, start, paced_pieces = by_half(EARLY), by_half(START), by_half(PACED)
+    tail = early - TAIL
     x_dev = z * 2 + 1 - x
     z_dev = (z + 1 - 2 * lax.rem(z, 2)) * 2 + x
     a_dev = (3 - z) * 2 + x
@@ -93,7 +98,7 @@
 
     def load(slot, layer):
         k, side = slot // 2, slot % 2
-        target = (k + upper * (3 - 2 * k)) * 2 + (x if side == MINE else 1 - x)
+        target = (k + upper * (3 - 2 * k)) * 2 + x + side * (1 - 2 * x)
         return pltpu.make_async_copy(
             grads.at[0, layer, pl.ds(target * rows, rows), :], held.at[slot, layer], load_sem.at[slot, layer]
         )
@@ -107,17 +112,20 @@
         pairs = ((params_in, params_out), (moment_in, moment_out), (second_in, second_out))
         return [pltpu.make_async_copy(src, dst, state_sem.at[i]) for i, (src, dst) in enumerate(pairs)]
 
+    raw = 3 - 2 * place
     load(7, 0).start()
-    for device in ({"dp": x_dev}, {"dp": z_dev}, {"mp": mp ^ 1}, {"mp": mp ^ 2}):
+    load(raw, 0).start()
+    for device in ({"dp": x_dev}, {"dp": z_dev}):
         greet(barrier, device)
 
     @pl.when(place == 1)
     def _():
-        greet(barrier, {"dp": a_dev})
+        for device in ({"dp": a_dev}, {"mp": mp ^ 1}, {"mp": mp ^ 2}):
+            greet(barrier, device)
 
     load(7, 1).start()
-    pl.when(place == 0)(lambda: fetch(3))
-    pl.when(place == 1)(lambda: fetch(1))
+    load(raw, 1).start()
+    fetch(6, 5, 4 - raw, 4, 2, 0)
 
     def loaded(*slots):
         for slot in slots:
@@ -134,15 +142,10 @@
         tile = jnp.where(lane == layers + layer, keep * losses[0, layer], tile)
     st0[dp] = tile
 
-    pl.when(place == 0)(lambda: pl.semaphore_wait(barrier, 4))
+    pl.when(place == 0)(lambda: pl.semaphore_wait(barrier, 2))
     pl.when(place == 1)(lambda: pl.semaphore_wait(barrier, 5))
 
     def meet():
-        greet(y_in, {"mp": mp ^ 2})
-        pl.semaphore_wait(y_in, 1)
-        greet(x_in, {"dp": x_dev})
-        pl.semaphore_wait(x_in, 1)
-
         @pl.when(place == 0)
         def _():
             greet(end_in, {"dp": z_dev})
@@ -151,6 +154,10 @@
         @pl.when(place == 1)
         def _():
             pl.semaphore_wait(end_in, 1)
+            greet(core_in, {"mp": mp ^ 1})
+            pl.semaphore_wait(core_in, 1)
+            greet(y_in, {"mp": mp ^ 2})
+            pl.semaphore_wait(y_in, 1)
             greet(middle_in, {"dp": a_dev})
             pl.semaphore_wait(middle_in, 1)
             greet(all_in, {"dp": z_dev})
@@ -222,22 +229,21 @@
     def _():
         load(7, 0).wait()
         x_own(3, 0)
+        load(3, 0).wait()
+
+        def z_raw(c):
+            snd[3, c] = own(3, c)
+            to_z(3, 0, c).start()
+
+        def first(c):
+            x_own(3, c)
+            pl.when(c < early)(lambda: z_raw(c))
+
+        z_raw(0)
+        each(1, per_layer, first)
         load(7, 1).wait()
-        loaded(3)
-
-        def first(c):
-            @pl.when(c > 0)
-            def _():
-                x_own(3, c)
-
-            @pl.when(c < early)
-            def _():
-                snd[3, c] = own(3, c)
-                to_z(3, 0, c).start()
-
-        each(0, 1, first)
-        fetch(6, 5, 1, 4, 2, 0)
-        each(1, pieces, first)
+        load(3, 1).wait()
+        each(per_layer, pieces, first)
         meet()
         for copy in state():
             copy.start()
@@ -288,21 +294,17 @@
     @pl.when(place == 1)
     def _():
         load(7, 0).wait()
-        x_own(3, 0)
-        load(7, 1).wait()
-        loaded(1)
+        load(1, 0).wait()
 
         def first(c):
-            @pl.when(c > 0)
-            def _():
-                x_own(3, c)
-
+            x_own(3, c)
             snd[1, c] = own(1, c)
             to_z(1, 1, c).start()
 
-        each(0, 1, first)
-        fetch(6, 5, 3, 4, 2, 0)
-        each(1, pieces, first)
+        each(0, per_layer, first)
+        load(7, 1).wait()
+        load(1, 1).wait()
+        each(per_layer, pieces, first)
         meet()
         for copy in state():
             copy.start()
@@ -359,6 +361,7 @@
 
     for copy in state():
         copy.wait()
+
     def weigh(ref, layer, c, factor):
         window = (layer, pl.ds(pl.multiple_of(c * depth, depth), depth))
         ref[window] = ref[window] * factor
@@ -381,54 +384,48 @@
     for layer in range(1, layers):
         weight_sum = weight_sum + weights[layer].astype(jnp.float32)
     square[...] = jnp.zeros_like(square)
-    factors = [weights[layer].astype(jnp.float32) / (weight_sum * total[:, layer : layer + 1]) for layer in range(layers)]
+    for layer in range(layers):
+        factor = weights[layer].astype(jnp.float32) / (weight_sum * total[:, layer : layer + 1])
+        factors[layer] = jnp.broadcast_to(factor, factors.shape[1:])
 
     def count(gradient):
         squares = gradient * gradient
         square[...] += jnp.sum(squares.reshape(depth // 8, 8, squares.shape[1]), axis=0)
 
-    def finish(layer, c, summed):
+    def finish(c, summed):
+        layer, r = c // per_layer, lax.rem(c, per_layer)
         gradient = summed * factors[layer]
-        r = lax.rem(c, per_layer)
         out[layer, pl.ds(pl.multiple_of(r * depth, depth), depth), :] = gradient
         return gradient
 
-    def spans(low, high):
-        cuts = [low, *(b for b in range(per_layer, pieces, per_layer) if low < b < high), high]
-        return [(a // per_layer, a, b) for a, b in zip(cuts, cuts[1:]) if a < b]
-
-    def last(c, layer):
-        return finish(layer, c, own(2, c) + from_x(1, c) + from_a(1, c) + from_z(1, c))
-
-    def finish_only(c, layer):
-        finish(layer, c, snd[2, c] + from_z(1, c))
-
-    def last_end(c, layer):
-        count(finish(layer, c, own(0, c) + from_z(0, c) + from_x(0, c)))
-
-    def count_tail(c, layer):
+    def last(c):
+        count(finish(c, own(2, c) + from_x(1, c) + from_a(1, c) + from_z(1, c)))
+
+    def finish_tail(c):
+        finish(c, snd[2, c] + from_z(1, c))
+
+    def last_end(c):
+        count(finish(c, own(0, c) + from_z(0, c) + from_x(0, c)))
+
+    def count_tail(c):
         snd[2, c] = own(2, c)
-        count((snd[2, c] + from_tail(c)) * factors[layer])
-
-    def paced(c, layer):
-        to_z(2, 1, c - START + tail).start()
-        last_end(c, layer)
-
-    def over(step, *ranges):
-        for low, high in ranges:
-            for layer, a, b in spans(low, high):
-                each(a, b, lambda c, layer=layer: step(c, layer))
+        count((snd[2, c] + from_tail(c)) * factors[c // per_layer])
+
+    def paced(c):
+        to_z(2, 1, c - start + tail).start()
+        last_end(c)
 
     @pl.when(place == 0)
     def _():
-        over(count_tail, (tail, early))
-        over(last_end, (0, START))
-        over(paced, (START, START + PACED))
-        over(last_end, (START + PACED, pieces))
+        each(tail, early, count_tail)
+        each(0, start, last_end)
+        each(start, start + paced_pieces, paced)
+        each(start + paced_pieces, pieces, last_end)
 
     @pl.when(place == 1)
     def _():
-        over(lambda c, layer: count(last(c, layer)), (early, pieces), (0, tail))
+        each(early, pieces, last)
+        each(0, tail, last)
 
     def share_square(i):
         return pltpu.make_async_remote_copy(
@@ -451,29 +448,20 @@
 
     @pl.when(place == 0)
     def _():
-        each(tail + PACED, early, lambda c: to_z(2, 1, c).start())
+        each(tail + paced_pieces, early, lambda c: to_z(2, 1, c).start())
 
     @pl.when(place == 1)
     def _():
-        over(finish_only, (tail, early))
-
-    for i in range(1, devices):
-        square_arrival(i).wait_recv()
-    all_rows = st1[0]
-    for i in range(1, devices):
-        all_rows = all_rows + st1[i]
-    square_sum = jnp.sum(all_rows, keepdims=True)
-    rms_value = jnp.sqrt(square_sum / entries)
-    clip_out[...] = jnp.broadcast_to(jnp.minimum(1.0, max_rms / (rms_value + eps_norm)), clip_out.shape)
+        each(tail, early, finish_tail)
 
     for i in range(1, 8):
         share_stats(i).wait_send()
     for i in range(1, devices):
         share_square(i).wait_send()
 
-    def sent(slot, low=0, high=pieces):
+    def sent(slot, size=pieces):
         pltpu.make_async_remote_copy(
-            src_ref=snd.at[slot, pl.ds(low, high - low)], dst_ref=zr.at[0, pl.ds(low, high - low)],
+            src_ref=snd.at[slot, pl.ds(0, size)], dst_ref=zr.at[0, pl.ds(0, size)],
             send_sem=send_sem.at[slot], recv_sem=z_sem.at[0, 0],
             device_id={"dp": z_dev}, device_id_type=MESH_ID,
         ).wait_send()
@@ -488,7 +476,13 @@
     @pl.when(place == 1)
     def _():
         sent(0)
-        sent(2, tail, early)
+        sent(2, TAIL)
+
+    for i in range(1, devices):
+        square_arrival(i).wait_recv()
+    square_sum = jnp.sum(jnp.sum(st1[...], axis=0), keepdims=True)
+    rms_value = jnp.sqrt(square_sum / entries)
+    clip_out[...] = jnp.broadcast_to(jnp.minimum(1.0, max_rms / (rms_value + eps_norm)), clip_out.shape)
 
 
 def update_kernel(gradient, params, moment, second, stats, clip, params_out, moment_out, second_out, mean_out, news, mean, sem, mean_sem):
@@ -562,6 +556,7 @@
             pltpu.VMEM((8, 1, LANES), f32),
             pltpu.VMEM((8 * n_mp, 1, LANES), f32),
             pltpu.VMEM((8, columns), f32),
+            pltpu.VMEM((layers, 1, columns), f32),
         ],
         compiler_params=pltpu.CompilerParams(
             collective_id=0, has_side_effects=True, vmem_limit_bytes=40 * 1024 * 1024

time: 91.3 us -> 88.9 us (0.974)
  Pallas kernels: 90.5 us -> 88.1 us
    pallas_call x1, Pallas kernels: 88.7 us -> 86.4 us  [line_body(): pl.pallas_call(kernel, name='line_reduce', out_shape=(state, state, state...]
where the time goes in v3:
time: 88.9 us; the launch traced here: 88.8 us
  Pallas kernels  88.1 us (99%)
    pallas_call x1, Pallas kernels, line_body(): pl.pallas_call(kernel, name='line_reduce', out_shape=(state, state, state...  86.4 us

profile of v3, /device:TPU:0, one launch (start us, length us, event | category | flops | bytes accessed | tf_op | source)
XLA Modules:
  0.0 88.8 jit_solution(6395112247210565957)
XLA Ops:
  0.6 86.4 %line_reduce.1 = (f32[2,512,256]{2,1,0:T(8,128)S(1)}, f32[2,512,256]{2,1,0:T(8,128)S(1)}, f32[2,512,256]{2,1,0:T(8,128)S(1)}, f32[2,512,256]{2,1,0:T(8,128)S(1)}...) custom-call(s32[1,2]{1,0:T(1,128)} %refs_0_.1, f32[1,2]{1,0:T(1,128)} %refs_1_.1, s32[2]{0:T(128)} %refs_2_.1, ...), custom_call_target="tpu_custom_call" | custom-call | tf_op jit(solution)/shard_map/line_reduce/pallas_call | solution.py:536
  87.1 1.7 %update.1 = (f32[2,512,256]{2,1,0:T(8,128)}, f32[2,512,256]{2,1,0:T(8,128)}, f32[2,512,256]{2,1,0:T(8,128)}, f32[1,2]{1,0:T(1,128)}) custom-call(f32[2,512,256]{2,1,0:T(8,128)S(1)} %get-tuple-element.14.gradient, f32[2,512,256]{2,1,0:T(8,128)S(1)} %get-tuple-element.15.params, f32[2,512,256]{2,1,0:T(8,128)S(1)} %get-tuple-element.16.moment, ...), custom_call_target="tpu_custom_call" | custom-call | tf_op jit(solution)/shard_map/update/pallas_call | solution.py:568

commit v4 on v3

--- a/solution.py
+++ b/solution.py
@@ -18,11 +18,12 @@
 LANES = 128
 LAG = 8
 EARLY = (18, 21)
-START = (18, 24)
-PACED = (11, 5)
-TAIL = 13
+START = (19, 25)
+PACED = (10, 4)
+TAIL = 12
+HEAD = 2
 CHUNK = 64
-STEP = 32
+STEP = 16
 MINE, OTHER = 0, 1
 
 
@@ -56,20 +57,13 @@
     n_mp, entries, mask_in, losses_in, weights_in, grads, params_in, moment_in, second_in,
     out, params_out, moment_out, second_out, stats_out, clip_out,
     mask, losses, weights, held, snd, xr, zr, ar, tr, st0, st1, square, factors,
-    small_sem, load_sem, state_sem, send_sem, x_sem, z_sem, a_sem, t_sem,
+    small_sem, head_sem, load_sem, state_sem, send_sem, x_sem, z_sem, a_sem, t_sem,
     st0_send, st0_recv, st1_send, st1_recv, end_in, core_in, y_in, middle_in, all_in,
 ):
     layers, rows = out.shape[0], out.shape[1]
     pieces = snd.shape[1]
     depth = snd.shape[2]
     per_layer = pieces // layers
-    small = [
-        pltpu.make_async_copy(src, dst, small_sem.at[i])
-        for i, (src, dst) in enumerate(((mask_in, mask), (losses_in, losses), (weights_in, weights)))
-    ]
-    for copy in small:
-        copy.start()
-
     dp, mp = lax.axis_index("dp"), lax.axis_index("mp")
     z, x = dp // 2, lax.rem(dp, 2)
     upper = z // 2
@@ -96,12 +90,40 @@
     def greet(sem, device):
         pl.semaphore_signal(sem, inc=1, device_id=device, device_id_type=MESH_ID)
 
-    def load(slot, layer):
+    greet(barrier, {"dp": x_dev})
+
+    def load(slot, layer, low=0, high=rows, sem=None):
         k, side = slot // 2, slot % 2
         target = (k + upper * (3 - 2 * k)) * 2 + x + side * (1 - 2 * x)
         return pltpu.make_async_copy(
-            grads.at[0, layer, pl.ds(target * rows, rows), :], held.at[slot, layer], load_sem.at[slot, layer]
+            grads.at[0, layer, pl.ds(target * rows + low, high - low), :],
+            held.at[slot, layer, pl.ds(low, high - low)],
+            load_sem.at[slot, layer] if sem is None else head_sem.at[sem],
         )
+
+    def load_head(i):
+        return load((7, raw)[i], 0, 0, HEAD * depth, i)
+
+    def load_body(i):
+        return load((7, raw)[i], 0, HEAD * depth)
+
+    raw = 3 - 2 * place
+    small = [
+        pltpu.make_async_copy(src, dst, small_sem.at[i])
+        for i, (src, dst) in enumerate(((mask_in, mask), (losses_in, losses), (weights_in, weights)))
+    ]
+    small[0].start()
+    load_head(0).start()
+    load_head(1).start()
+    greet(barrier, {"dp": z_dev})
+
+    @pl.when(place == 1)
+    def _():
+        for device in ({"dp": a_dev}, {"mp": mp ^ 1}, {"mp": mp ^ 2}):
+            greet(barrier, device)
+
+    load_body(0).start()
+    load_body(1).start()
 
     def fetch(*slots):
         for slot in slots:
@@ -112,38 +134,31 @@
         pairs = ((params_in, params_out), (moment_in, moment_out), (second_in, second_out))
         return [pltpu.make_async_copy(src, dst, state_sem.at[i]) for i, (src, dst) in enumerate(pairs)]
 
-    raw = 3 - 2 * place
-    load(7, 0).start()
-    load(raw, 0).start()
-    for device in ({"dp": x_dev}, {"dp": z_dev}):
-        greet(barrier, device)
-
-    @pl.when(place == 1)
-    def _():
-        for device in ({"dp": a_dev}, {"mp": mp ^ 1}, {"mp": mp ^ 2}):
-            greet(barrier, device)
-
     load(7, 1).start()
     load(raw, 1).start()
     fetch(6, 5, 4 - raw, 4, 2, 0)
+    for copy in small[1:]:
+        copy.start()
 
     def loaded(*slots):
         for slot in slots:
             for layer in range(layers):
                 load(slot, layer).wait()
 
-    for copy in small:
-        copy.wait()
-    lane = lax.broadcasted_iota(jnp.int32, st0.shape[1:], 1)
-    tile = jnp.zeros(st0.shape[1:], jnp.float32)
-    for layer in range(layers):
-        keep = mask[0, layer].astype(jnp.float32)
-        tile = jnp.where(lane == layer, keep, tile)
-        tile = jnp.where(lane == layers + layer, keep * losses[0, layer], tile)
-    st0[dp] = tile
-
+    small[0].wait()
     pl.when(place == 0)(lambda: pl.semaphore_wait(barrier, 2))
     pl.when(place == 1)(lambda: pl.semaphore_wait(barrier, 5))
+
+    def set_stats():
+        for copy in small[1:]:
+            copy.wait()
+        lane = lax.broadcasted_iota(jnp.int32, st0.shape[1:], 1)
+        tile = jnp.zeros(st0.shape[1:], jnp.float32)
+        for layer in range(layers):
+            keep = mask[0, layer].astype(jnp.float32)
+            tile = jnp.where(lane == layer, keep, tile)
+            tile = jnp.where(lane == layers + layer, keep * losses[0, layer], tile)
+        st0[dp] = tile
 
     def meet():
         @pl.when(place == 0)
@@ -227,10 +242,6 @@
 
     @pl.when(place == 0)
     def _():
-        load(7, 0).wait()
-        x_own(3, 0)
-        load(3, 0).wait()
-
         def z_raw(c):
             snd[3, c] = own(3, c)
             to_z(3, 0, c).start()
@@ -239,8 +250,14 @@
             x_own(3, c)
             pl.when(c < early)(lambda: z_raw(c))
 
+        load_head(0).wait()
+        x_own(3, 0)
+        load_head(1).wait()
         z_raw(0)
-        each(1, per_layer, first)
+        each(1, HEAD, first)
+        load_body(0).wait()
+        load_body(1).wait()
+        each(HEAD, per_layer, first)
         load(7, 1).wait()
         load(3, 1).wait()
         each(per_layer, pieces, first)
@@ -248,6 +265,7 @@
         for copy in state():
             copy.start()
         loaded(1, 6, 5)
+        set_stats()
         for i in range(1, 8):
             share_stats(i).start()
 
@@ -293,15 +311,18 @@
 
     @pl.when(place == 1)
     def _():
-        load(7, 0).wait()
-        load(1, 0).wait()
+        load_head(0).wait()
+        load_head(1).wait()
 
         def first(c):
             x_own(3, c)
             snd[1, c] = own(1, c)
             to_z(1, 1, c).start()
 
-        each(0, per_layer, first)
+        each(0, HEAD, first)
+        load_body(0).wait()
+        load_body(1).wait()
+        each(HEAD, per_layer, first)
         load(7, 1).wait()
         load(1, 1).wait()
         each(per_layer, pieces, first)
@@ -309,6 +330,7 @@
         for copy in state():
             copy.start()
         loaded(3, 6, 5)
+        set_stats()
         for i in range(1, 8):
             share_stats(i).start()
         loaded(4, 2, 0)
@@ -450,10 +472,6 @@
     def _():
         each(tail + paced_pieces, early, lambda c: to_z(2, 1, c).start())
 
-    @pl.when(place == 1)
-    def _():
-        each(tail, early, finish_tail)
-
     for i in range(1, 8):
         share_stats(i).wait_send()
     for i in range(1, devices):
@@ -483,6 +501,10 @@
     square_sum = jnp.sum(jnp.sum(st1[...], axis=0), keepdims=True)
     rms_value = jnp.sqrt(square_sum / entries)
     clip_out[...] = jnp.broadcast_to(jnp.minimum(1.0, max_rms / (rms_value + eps_norm)), clip_out.shape)
+
+    @pl.when(place == 1)
+    def _():
+        each(tail, early, finish_tail)
 
 
 def update_kernel(gradient, params, moment, second, stats, clip, params_out, moment_out, second_out, mean_out, news, mean, sem, mean_sem):
@@ -529,7 +551,7 @@
 
     def kernel(*refs):
         pl.run_scoped(lambda *sems: line_kernel(n_mp, entries, *refs, *sems),
-            dma((3,)), dma((8, layers)), dma((3,)), dma((8,)), dma((4, pieces)), dma((4, pieces)), dma((2, pieces)), dma((TAIL,)),
+            dma((3,)), dma((2,)), dma((8, layers)), dma((3,)), dma((8,)), dma((4, pieces)), dma((4, pieces)), dma((2, pieces)), dma((TAIL,)),
             dma((8,)), dma((8,)), dma((8 * n_mp,)), dma((8 * n_mp,)), regular, regular, regular, regular, regular,
         )
 

time: 88.9 us -> 88.9 us (level)
  no operation moved by 1% of the time
where the time goes in v4:
time: 88.9 us; the launch traced here: 88.8 us
  Pallas kernels  88.1 us (99%)
    pallas_call x1, Pallas kernels, line_body(): pl.pallas_call(kernel, name='line_reduce', out_shape=(state, state, state...  86.4 us

profile of v4, /device:TPU:0, one launch (start us, length us, event | category | flops | bytes accessed | tf_op | source)
XLA Modules:
  0.0 88.8 jit_solution(5512889045363543539)
XLA Ops:
  0.6 86.4 %line_reduce.1 = (f32[2,512,256]{2,1,0:T(8,128)S(1)}, f32[2,512,256]{2,1,0:T(8,128)S(1)}, f32[2,512,256]{2,1,0:T(8,128)S(1)}, f32[2,512,256]{2,1,0:T(8,128)S(1)}...) custom-call(s32[1,2]{1,0:T(1,128)} %refs_0_.1, f32[1,2]{1,0:T(1,128)} %refs_1_.1, s32[2]{0:T(128)} %refs_2_.1, ...), custom_call_target="tpu_custom_call" | custom-call | tf_op jit(solution)/shard_map/line_reduce/pallas_call | solution.py:558
  87.1 1.7 %update.1 = (f32[2,512,256]{2,1,0:T(8,128)}, f32[2,512,256]{2,1,0:T(8,128)}, f32[2,512,256]{2,1,0:T(8,128)}, f32[1,2]{1,0:T(1,128)}) custom-call(f32[2,512,256]{2,1,0:T(8,128)S(1)} %get-tuple-element.14.gradient, f32[2,512,256]{2,1,0:T(8,128)S(1)} %get-tuple-element.15.params, f32[2,512,256]{2,1,0:T(8,128)S(1)} %get-tuple-element.16.moment, ...), custom_call_target="tpu_custom_call" | custom-call | tf_op jit(solution)/shard_map/update/pallas_call | solution.py:590

commit v5 on v4

--- a/solution.py
+++ b/solution.py
@@ -15,12 +15,13 @@
 
 MESH_ID = pl.DeviceIdType.MESH
 ROWS = 32
+PIECES = 32
 LANES = 128
 LAG = 8
 EARLY = (18, 21)
-START = (19, 25)
-PACED = (10, 4)
-TAIL = 12
+START = (18, 24)
+PACED = (11, 5)
+TAIL = 13
 HEAD = 2
 CHUNK = 64
 STEP = 16
@@ -90,8 +91,6 @@
     def greet(sem, device):
         pl.semaphore_signal(sem, inc=1, device_id=device, device_id_type=MESH_ID)
 
-    greet(barrier, {"dp": x_dev})
-
     def load(slot, layer, low=0, high=rows, sem=None):
         k, side = slot // 2, slot % 2
         target = (k + upper * (3 - 2 * k)) * 2 + x + side * (1 - 2 * x)
@@ -115,6 +114,7 @@
     small[0].start()
     load_head(0).start()
     load_head(1).start()
+    greet(barrier, {"dp": x_dev})
     greet(barrier, {"dp": z_dev})
 
     @pl.when(place == 1)
@@ -609,7 +609,7 @@
         layers = args[4].shape[0]
 
         def body(*blocks):
-            if n_dp == 8 and n_mp == 4 and layers == 2:
+            if n_dp == 8 and n_mp == 4 and layers == 2 and entries == 8 * n_mp * PIECES * ROWS * 256:
                 return line_body(n_mp, entries, *blocks)
             return any_mesh_body(entries, *blocks)
 

time: 88.9 us -> 88.9 us (level)
  no operation moved by 1% of the time
where the time goes in v5:
time: 88.9 us; the launch traced here: 88.8 us
  Pallas kernels  88.1 us (99%)
    pallas_call x1, Pallas kernels, line_body(): pl.pallas_call(kernel, name='line_reduce', out_shape=(state, state, state...  86.4 us

profile of v5, /device:TPU:0, one launch (start us, length us, event | category | flops | bytes accessed | tf_op | source)
XLA Modules:
  0.0 88.8 jit_solution(5289518983140217991)
XLA Ops:
  0.6 86.4 %line_reduce.1 = (f32[2,512,256]{2,1,0:T(8,128)S(1)}, f32[2,512,256]{2,1,0:T(8,128)S(1)}, f32[2,512,256]{2,1,0:T(8,128)S(1)}, f32[2,512,256]{2,1,0:T(8,128)S(1)}...) custom-call(s32[1,2]{1,0:T(1,128)} %refs_0_.1, f32[1,2]{1,0:T(1,128)} %refs_1_.1, s32[2]{0:T(128)} %refs_2_.1, ...), custom_call_target="tpu_custom_call" | custom-call | tf_op jit(solution)/shard_map/line_reduce/pallas_call | solution.py:558
  87.1 1.7 %update.1 = (f32[2,512,256]{2,1,0:T(8,128)}, f32[2,512,256]{2,1,0:T(8,128)}, f32[2,512,256]{2,1,0:T(8,128)}, f32[1,2]{1,0:T(1,128)}) custom-call(f32[2,512,256]{2,1,0:T(8,128)S(1)} %get-tuple-element.14.gradient, f32[2,512,256]{2,1,0:T(8,128)S(1)} %get-tuple-element.15.params, f32[2,512,256]{2,1,0:T(8,128)S(1)} %get-tuple-element.16.moment, ...), custom_call_target="tpu_custom_call" | custom-call | tf_op jit(solution)/shard_map/update/pallas_call | solution.py:590

commit v6 on v4

--- a/solution.py
+++ b/solution.py
@@ -14,14 +14,14 @@
 decay_rate = 0.1
 
 MESH_ID = pl.DeviceIdType.MESH
-ROWS = 32
+ROWS = 64
 LANES = 128
-LAG = 8
-EARLY = (18, 21)
-START = (19, 25)
-PACED = (10, 4)
-TAIL = 12
-HEAD = 2
+LAG = 4
+EARLY = (9, 11)
+START = (10, 12)
+PACED = (5, 2)
+TAIL = 7
+GROUP = 4
 CHUNK = 64
 STEP = 16
 MINE, OTHER = 0, 1
@@ -57,7 +57,7 @@
     n_mp, entries, mask_in, losses_in, weights_in, grads, params_in, moment_in, second_in,
     out, params_out, moment_out, second_out, stats_out, clip_out,
     mask, losses, weights, held, snd, xr, zr, ar, tr, st0, st1, square, factors,
-    small_sem, head_sem, load_sem, state_sem, send_sem, x_sem, z_sem, a_sem, t_sem,
+    small_sem, head_sem, load_sem, state_sem, send_sem, xg_sem, zg_sem, x_sem, z_sem, a_sem,
     st0_send, st0_recv, st1_send, st1_recv, end_in, core_in, y_in, middle_in, all_in,
 ):
     layers, rows = out.shape[0], out.shape[1]
@@ -90,7 +90,13 @@
     def greet(sem, device):
         pl.semaphore_signal(sem, inc=1, device_id=device, device_id_type=MESH_ID)
 
-    greet(barrier, {"dp": x_dev})
+    for device in ({"dp": x_dev}, {"dp": z_dev}):
+        greet(barrier, device)
+
+    @pl.when(place == 1)
+    def _():
+        for device in ({"dp": a_dev}, {"mp": mp ^ 1}, {"mp": mp ^ 2}):
+            greet(barrier, device)
 
     def load(slot, layer, low=0, high=rows, sem=None):
         k, side = slot // 2, slot % 2
@@ -98,37 +104,36 @@
         return pltpu.make_async_copy(
             grads.at[0, layer, pl.ds(target * rows + low, high - low), :],
             held.at[slot, layer, pl.ds(low, high - low)],
-            load_sem.at[slot, layer] if sem is None else head_sem.at[sem],
+            load_sem.at[slot] if sem is None else head_sem.at[sem],
         )
 
     def load_head(i):
-        return load((7, raw)[i], 0, 0, HEAD * depth, i)
+        return load((7, raw)[i], 0, 0, GROUP * depth, i)
 
     def load_body(i):
-        return load((7, raw)[i], 0, HEAD * depth)
+        return load((7, raw)[i], 0, GROUP * depth, rows, 2 + i)
+
+    def load_slot(slot):
+        k, side = slot // 2, slot % 2
+        target = (k + upper * (3 - 2 * k)) * 2 + x + side * (1 - 2 * x)
+        return pltpu.make_async_copy(grads.at[0, :, pl.ds(target * rows, rows), :], held.at[slot], load_sem.at[slot])
 
     raw = 3 - 2 * place
     small = [
         pltpu.make_async_copy(src, dst, small_sem.at[i])
         for i, (src, dst) in enumerate(((mask_in, mask), (losses_in, losses), (weights_in, weights)))
     ]
-    small[0].start()
+    for copy in small:
+        copy.start()
     load_head(0).start()
     load_head(1).start()
-    greet(barrier, {"dp": z_dev})
-
-    @pl.when(place == 1)
-    def _():
-        for device in ({"dp": a_dev}, {"mp": mp ^ 1}, {"mp": mp ^ 2}):
-            greet(barrier, device)
 
     load_body(0).start()
     load_body(1).start()
 
     def fetch(*slots):
         for slot in slots:
-            for layer in range(layers):
-                load(slot, layer).start()
+            load_slot(slot).start()
 
     def state():
         pairs = ((params_in, params_out), (moment_in, moment_out), (second_in, second_out))
@@ -137,28 +142,23 @@
     load(7, 1).start()
     load(raw, 1).start()
     fetch(6, 5, 4 - raw, 4, 2, 0)
-    for copy in small[1:]:
-        copy.start()
 
     def loaded(*slots):
         for slot in slots:
-            for layer in range(layers):
-                load(slot, layer).wait()
-
-    small[0].wait()
+            load_slot(slot).wait()
+
+    for copy in small:
+        copy.wait()
+    lane = lax.broadcasted_iota(jnp.int32, st0.shape[1:], 1)
+    tile = jnp.zeros(st0.shape[1:], jnp.float32)
+    for layer in range(layers):
+        keep = mask[0, layer].astype(jnp.float32)
+        tile = jnp.where(lane == layer, keep, tile)
+        tile = jnp.where(lane == layers + layer, keep * losses[0, layer], tile)
+    st0[dp] = tile
+
     pl.when(place == 0)(lambda: pl.semaphore_wait(barrier, 2))
     pl.when(place == 1)(lambda: pl.semaphore_wait(barrier, 5))
-
-    def set_stats():
-        for copy in small[1:]:
-            copy.wait()
-        lane = lax.broadcasted_iota(jnp.int32, st0.shape[1:], 1)
-        tile = jnp.zeros(st0.shape[1:], jnp.float32)
-        for layer in range(layers):
-            keep = mask[0, layer].astype(jnp.float32)
-            tile = jnp.where(lane == layer, keep, tile)
-            tile = jnp.where(lane == layers + layer, keep * losses[0, layer], tile)
-        st0[dp] = tile
 
     def meet():
         @pl.when(place == 0)
@@ -182,9 +182,9 @@
         keep = mask[0, layer].astype(jnp.float32)
         return held[slot, layer, pl.ds(pl.multiple_of(r * depth, depth), depth), :].astype(jnp.float32) * keep
 
-    def push(slot, c, dst, sem, device):
+    def push(slot, c, dst, sem, device, count=None):
         return pltpu.make_async_remote_copy(
-            src_ref=snd.at[slot, c], dst_ref=dst, send_sem=send_sem.at[slot], recv_sem=sem,
+            src_ref=snd.at[slot, c if count is None else pl.ds(c, count)], dst_ref=dst, send_sem=send_sem.at[slot], recv_sem=sem,
             device_id={"dp": device}, device_id_type=MESH_ID,
         )
 
@@ -194,11 +194,17 @@
     def to_z(slot, box, c):
         return push(slot, c, zr.at[box, c], z_sem.at[box, c], z_dev)
 
+    def group_to_x(k, c):
+        return push(2 * k + OTHER, c, xr.at[k, pl.ds(c, GROUP)], xg_sem.at[k - 2, c // GROUP], x_dev, GROUP)
+
+    def group_to_z(k, c):
+        return push(2 * k + MINE, c, zr.at[k, pl.ds(c, GROUP)], zg_sem.at[k - 2, c // GROUP], z_dev, GROUP)
+
     def to_a(k, c):
         return push(2 * k + MINE, c, ar.at[3 - k, c], a_sem.at[3 - k, c], a_dev)
 
     def to_tail(c):
-        return push(2, c, tr.at[c - tail], t_sem.at[c - tail], z_dev)
+        return push(2, c, tr.at[c - tail], a_sem.at[0, c - tail], z_dev)
 
     def from_tail(c):
         to_tail(c).wait_recv()
@@ -227,17 +233,24 @@
         snd[2 * k + OTHER, c] = own(2 * k + OTHER, c)
         to_x(k, c).start()
 
+    def x_group(k, c):
+        for i in range(GROUP):
+            snd[2 * k + OTHER, c + i] = own(2 * k + OTHER, c + i)
+        group_to_x(k, c).start()
+
+    def groups(low, high, step):
+        each(low // GROUP, high // GROUP, lambda g: step(g * GROUP))
+
     def share_stats(i):
         return pltpu.make_async_remote_copy(
-            src_ref=st0.at[dp], dst_ref=st0.at[dp], send_sem=st0_send.at[i], recv_sem=st0_recv.at[dp],
+            src_ref=st0.at[dp], dst_ref=st0.at[dp], send_sem=st0_send, recv_sem=st0_recv,
             device_id={"dp": lax.rem(dp + i, 8)}, device_id_type=MESH_ID,
         )
 
-    def stats_arrival(i):
-        peer = lax.rem(dp + i, 8)
+    def all_stats():
         return pltpu.make_async_remote_copy(
-            src_ref=st0.at[dp], dst_ref=st0.at[peer], send_sem=st0_send.at[i], recv_sem=st0_recv.at[peer],
-            device_id={"dp": peer}, device_id_type=MESH_ID,
+            src_ref=st0.at[pl.ds(0, 7)], dst_ref=st0.at[pl.ds(0, 7)], send_sem=st0_send, recv_sem=st0_recv,
+            device_id={"dp": x_dev}, device_id_type=MESH_ID,
         )
 
     @pl.when(place == 0)
@@ -247,34 +260,39 @@
             to_z(3, 0, c).start()
 
         def first(c):
-            x_own(3, c)
-            pl.when(c < early)(lambda: z_raw(c))
+            x_group(3, c)
+            for i in range(GROUP):
+                pl.when(c + i < early)(lambda: z_raw(c + i))
 
         load_head(0).wait()
-        x_own(3, 0)
+        x_group(3, 0)
         load_head(1).wait()
-        z_raw(0)
-        each(1, HEAD, first)
+        for i in range(GROUP):
+            z_raw(i)
         load_body(0).wait()
         load_body(1).wait()
-        each(HEAD, per_layer, first)
+        groups(GROUP, per_layer, first)
         load(7, 1).wait()
         load(3, 1).wait()
-        each(per_layer, pieces, first)
+        groups(per_layer, pieces, first)
         meet()
         for copy in state():
             copy.start()
         loaded(1, 6, 5)
-        set_stats()
         for i in range(1, 8):
             share_stats(i).start()
 
+        def pass_on(k, c):
+            group_to_x(k, c).wait_recv()
+            for i in range(GROUP):
+                snd[2 * k, c + i] = own(2 * k, c + i) + xr[k, c + i]
+            group_to_z(k, c).start()
+
         def second(c):
-            snd[6, c] = own(6, c) + from_x(3, c)
-            to_z(6, 3, c).start()
-            x_own(2, c)
-
-        each(0, pieces, second)
+            pass_on(3, c)
+            x_group(2, c)
+
+        groups(0, pieces, second)
         loaded(4, 2, 0)
 
         def send_own_level(c):
@@ -282,19 +300,12 @@
             to_x(0, c).start()
 
         def third(c):
-            snd[4, c] = own(4, c) + from_x(2, c)
-            to_z(4, 2, c).start()
-
-        def third_a(c):
-            third(c)
-            x_own(1, c + early)
-
-        def third_b(c):
-            third(c)
-            send_own_level(c - (pieces - early))
-
-        each(0, pieces - early, third_a)
-        each(pieces - early, pieces, third_b)
+            pass_on(2, c)
+            for i in range(GROUP):
+                pl.when(c + i < pieces - early)(lambda: x_own(1, c + i + early))
+                pl.when(c + i >= pieces - early)(lambda: send_own_level(c + i - (pieces - early)))
+
+        groups(0, pieces, third)
 
         def fourth(c):
             snd[2, c] = own(2, c) + from_x(1, c)
@@ -315,22 +326,22 @@
         load_head(1).wait()
 
         def first(c):
-            x_own(3, c)
-            snd[1, c] = own(1, c)
-            to_z(1, 1, c).start()
-
-        each(0, HEAD, first)
+            x_group(3, c)
+            for i in range(GROUP):
+                snd[1, c + i] = own(1, c + i)
+                to_z(1, 1, c + i).start()
+
+        groups(0, GROUP, first)
         load_body(0).wait()
         load_body(1).wait()
-        each(HEAD, per_layer, first)
+        groups(GROUP, per_layer, first)
         load(7, 1).wait()
         load(1, 1).wait()
-        each(per_layer, pieces, first)
+        groups(per_layer, pieces, first)
         meet()
         for copy in state():
             copy.start()
         loaded(3, 6, 5)
-        set_stats()
         for i in range(1, 8):
             share_stats(i).start()
         loaded(4, 2, 0)
@@ -339,47 +350,41 @@
             snd[0, c] = own(0, c) + from_a(0, c)
             to_z(0, 0, c).start()
 
+        def merge(k, c):
+            group_to_x(k, c).wait_recv()
+            group_to_z(k, c).wait_recv()
+            for i in range(GROUP):
+                snd[2 * k, c + i] = own(2 * k, c + i) + xr[k, c + i] + zr[k, c + i]
+                to_a(k, c + i).start()
+
+        def x_early(c):
+            snd[3, c] = own(3, c) + from_z(0, c)
+            to_x(1, c).start()
+
         def second(c):
-            x_own(2, c)
-
-            @pl.when(c < early)
-            def _():
-                snd[3, c] = own(3, c) + from_z(0, c)
-                to_x(1, c).start()
-
-            snd[6, c] = own(6, c) + from_x(3, c) + from_z(3, c)
-            to_a(3, c).start()
-
-        def second_b(c):
-            second(c)
-            pass_out(c - LAG)
-
-        each(0, LAG, second)
-        each(LAG, pieces, second_b)
-
-        def third(c):
-            @pl.when(c < pieces - early)
-            def _():
-                x_own(1, c + early)
-
-            snd[4, c] = own(4, c) + from_x(2, c) + from_z(2, c)
-            to_a(2, c).start()
-
-            @pl.when(c < LAG)
-            def _():
-                pass_out(c + pieces - LAG)
+            x_group(2, c)
+            for i in range(GROUP):
+                pl.when(c + i < early)(lambda: x_early(c + i))
+            merge(3, c)
+            for i in range(GROUP):
+                pl.when(c >= LAG)(lambda: pass_out(c + i - LAG))
+
+        groups(0, pieces, second)
 
         def return_tail(c):
             snd[2, c] = own(2, c) + from_x(1, c) + from_a(1, c)
             to_tail(c).start()
 
-        def third_b(c):
-            third(c)
-            return_tail(c - LAG)
-
-        each(0, tail + LAG, third)
-        each(tail + LAG, early + LAG, third_b)
-        each(early + LAG, pieces, third)
+        def third(c):
+            for i in range(GROUP):
+                pl.when(c + i < pieces - early)(lambda: x_own(1, c + i + early))
+            merge(2, c)
+            for i in range(GROUP):
+                late = c + i - LAG
+                pl.when(c < LAG)(lambda: pass_out(late + pieces))
+                pl.when((late >= tail) & (late < early))(lambda: return_tail(late))
+
+        groups(0, pieces, third)
 
     for copy in state():
         copy.wait()
@@ -396,8 +401,7 @@
 
         each(0, per_layer, weigh_all)
 
-    for i in range(1, 8):
-        stats_arrival(i).wait_recv()
+    all_stats().wait_recv()
     total = st0[0]
     for i in range(1, 8):
         total = total + st0[i]
@@ -452,15 +456,14 @@
     def share_square(i):
         return pltpu.make_async_remote_copy(
             src_ref=st1.at[place_in_all], dst_ref=st1.at[place_in_all],
-            send_sem=st1_send.at[i], recv_sem=st1_recv.at[place_in_all],
+            send_sem=st1_send, recv_sem=st1_recv,
             device_id=away(i)[1], device_id_type=MESH_ID,
         )
 
-    def square_arrival(i):
-        peer, device = away(i)
+    def all_squares():
         return pltpu.make_async_remote_copy(
-            src_ref=st1.at[place_in_all], dst_ref=st1.at[peer], send_sem=st1_send.at[i], recv_sem=st1_recv.at[peer],
-            device_id=device, device_id_type=MESH_ID,
+            src_ref=st1.at[pl.ds(0, devices - 1)], dst_ref=st1.at[pl.ds(0, devices - 1)],
+            send_sem=st1_send, recv_sem=st1_recv, device_id={"dp": x_dev}, device_id_type=MESH_ID,
         )
 
     folded = jnp.sum(square[...], axis=0, keepdims=True)
@@ -472,10 +475,8 @@
     def _():
         each(tail + paced_pieces, early, lambda c: to_z(2, 1, c).start())
 
-    for i in range(1, 8):
-        share_stats(i).wait_send()
-    for i in range(1, devices):
-        share_square(i).wait_send()
+    all_stats().wait_send()
+    all_squares().wait_send()
 
     def sent(slot, size=pieces):
         pltpu.make_async_remote_copy(
@@ -496,8 +497,7 @@
         sent(0)
         sent(2, TAIL)
 
-    for i in range(1, devices):
-        square_arrival(i).wait_recv()
+    all_squares().wait_recv()
     square_sum = jnp.sum(jnp.sum(st1[...], axis=0), keepdims=True)
     rms_value = jnp.sqrt(square_sum / entries)
     clip_out[...] = jnp.broadcast_to(jnp.minimum(1.0, max_rms / (rms_value + eps_norm)), clip_out.shape)
@@ -550,10 +550,7 @@
     state = jax.ShapeDtypeStruct((layers, rows, columns), f32)
 
     def kernel(*refs):
-        pl.run_scoped(lambda *sems: line_kernel(n_mp, entries, *refs, *sems),
-            dma((3,)), dma((2,)), dma((8, layers)), dma((3,)), dma((8,)), dma((4, pieces)), dma((4, pieces)), dma((2, pieces)), dma((TAIL,)),
-            dma((8,)), dma((8,)), dma((8 * n_mp,)), dma((8 * n_mp,)), regular, regular, regular, regular, regular,
-        )
+        line_kernel(n_mp, entries, *refs)
 
     *held, stats, clip = pl.pallas_call(
         kernel,
@@ -579,6 +576,9 @@
             pltpu.VMEM((8 * n_mp, 1, LANES), f32),
             pltpu.VMEM((8, columns), f32),
             pltpu.VMEM((layers, 1, columns), f32),
+            dma((3,)), dma((4,)), dma((8,)), dma((3,)), dma((8,)), dma((2, pieces // GROUP)), dma((2, pieces // GROUP)),
+            dma((2, pieces)), dma((2, pieces)), dma((2, pieces)), dma, dma, dma, dma,
+            regular, regular, regular, regular, regular,
         ],
         compiler_params=pltpu.CompilerParams(
             collective_id=0, has_side_effects=True, vmem_limit_bytes=40 * 1024 * 1024

time: 88.9 us -> 90.6 us (1.019); the launches traced: 88.8 us -> 89.5 us
  no operation moved by 1% of the time
where the time goes in v6:
time: 90.6 us; the launch traced here: 89.5 us
  Pallas kernels  88.9 us (98%)
    pallas_call x1, Pallas kernels, line_body(): pl.pallas_call(kernel, name='line_reduce', out_shape=(state, state, state...  87.2 us

profile of v6, /device:TPU:0, one launch (start us, length us, event | category | flops | bytes accessed | tf_op | source)
XLA Modules:
  0.0 89.5 jit_solution(2192466187626934242)
XLA Ops:
  0.6 87.2 %line_reduce.1 = (f32[2,512,256]{2,1,0:T(8,128)S(1)}, f32[2,512,256]{2,1,0:T(8,128)S(1)}, f32[2,512,256]{2,1,0:T(8,128)S(1)}, f32[2,512,256]{2,1,0:T(8,128)S(1)}...) custom-call(s32[1,2]{1,0:T(1,128)} %refs_0_.1, f32[1,2]{1,0:T(1,128)} %refs_1_.1, s32[2]{0:T(128)} %refs_2_.1, ...), custom_call_target="tpu_custom_call" | custom-call | tf_op jit(solution)/shard_map/line_reduce/pallas_call | solution.py:555
  87.8 1.7 %update.1 = (f32[2,512,256]{2,1,0:T(8,128)}, f32[2,512,256]{2,1,0:T(8,128)}, f32[2,512,256]{2,1,0:T(8,128)}, f32[1,2]{1,0:T(1,128)}) custom-call(f32[2,512,256]{2,1,0:T(8,128)S(1)} %get-tuple-element.14.gradient, f32[2,512,256]{2,1,0:T(8,128)S(1)} %get-tuple-element.15.params, f32[2,512,256]{2,1,0:T(8,128)S(1)} %get-tuple-element.16.moment, ...), custom_call_target="tpu_custom_call" | custom-call | tf_op jit(solution)/shard_map/update/pallas_call | solution.py:590

commit v7 on v4

--- a/solution.py
+++ b/solution.py
@@ -15,6 +15,7 @@
 
 MESH_ID = pl.DeviceIdType.MESH
 ROWS = 32
+PIECES = 32
 LANES = 128
 LAG = 8
 EARLY = (18, 21)
@@ -90,8 +91,6 @@
     def greet(sem, device):
         pl.semaphore_signal(sem, inc=1, device_id=device, device_id_type=MESH_ID)
 
-    greet(barrier, {"dp": x_dev})
-
     def load(slot, layer, low=0, high=rows, sem=None):
         k, side = slot // 2, slot % 2
         target = (k + upper * (3 - 2 * k)) * 2 + x + side * (1 - 2 * x)
@@ -115,6 +114,7 @@
     small[0].start()
     load_head(0).start()
     load_head(1).start()
+    greet(barrier, {"dp": x_dev})
     greet(barrier, {"dp": z_dev})
 
     @pl.when(place == 1)
@@ -452,15 +452,14 @@
     def share_square(i):
         return pltpu.make_async_remote_copy(
             src_ref=st1.at[place_in_all], dst_ref=st1.at[place_in_all],
-            send_sem=st1_send.at[i], recv_sem=st1_recv.at[place_in_all],
+            send_sem=st1_send, recv_sem=st1_recv,
             device_id=away(i)[1], device_id_type=MESH_ID,
         )
 
-    def square_arrival(i):
-        peer, device = away(i)
+    def all_squares():
         return pltpu.make_async_remote_copy(
-            src_ref=st1.at[place_in_all], dst_ref=st1.at[peer], send_sem=st1_send.at[i], recv_sem=st1_recv.at[peer],
-            device_id=device, device_id_type=MESH_ID,
+            src_ref=st1.at[pl.ds(0, devices - 1)], dst_ref=st1.at[pl.ds(0, devices - 1)],
+            send_sem=st1_send, recv_sem=st1_recv, device_id={"dp": x_dev}, device_id_type=MESH_ID,
         )
 
     folded = jnp.sum(square[...], axis=0, keepdims=True)
@@ -474,8 +473,7 @@
 
     for i in range(1, 8):
         share_stats(i).wait_send()
-    for i in range(1, devices):
-        share_square(i).wait_send()
+    all_squares().wait_send()
 
     def sent(slot, size=pieces):
         pltpu.make_async_remote_copy(
@@ -496,8 +494,7 @@
         sent(0)
         sent(2, TAIL)
 
-    for i in range(1, devices):
-        square_arrival(i).wait_recv()
+    all_squares().wait_recv()
     square_sum = jnp.sum(jnp.sum(st1[...], axis=0), keepdims=True)
     rms_value = jnp.sqrt(square_sum / entries)
     clip_out[...] = jnp.broadcast_to(jnp.minimum(1.0, max_rms / (rms_value + eps_norm)), clip_out.shape)
@@ -552,7 +549,7 @@
     def kernel(*refs):
         pl.run_scoped(lambda *sems: line_kernel(n_mp, entries, *refs, *sems),
             dma((3,)), dma((2,)), dma((8, layers)), dma((3,)), dma((8,)), dma((4, pieces)), dma((4, pieces)), dma((2, pieces)), dma((TAIL,)),
-            dma((8,)), dma((8,)), dma((8 * n_mp,)), dma((8 * n_mp,)), regular, regular, regular, regular, regular,
+            dma((8,)), dma((8,)), dma, dma, regular, regular, regular, regular, regular,
         )
 
     *held, stats, clip = pl.pallas_call(
@@ -609,7 +606,7 @@
         layers = args[4].shape[0]
 
         def body(*blocks):
-            if n_dp == 8 and n_mp == 4 and layers == 2:
+            if n_dp == 8 and n_mp == 4 and layers == 2 and entries == 8 * n_mp * PIECES * ROWS * 256:
                 return line_body(n_mp, entries, *blocks)
             return any_mesh_body(entries, *blocks)
 

time: 88.9 us -> 88.9 us (level)
  no operation moved by 1% of the time
where the time goes in v7:
time: 88.9 us; the launch traced here: 88.8 us
  Pallas kernels  88.1 us (99%)
    pallas_call x1, Pallas kernels, line_body(): pl.pallas_call(kernel, name='line_reduce', out_shape=(state, state, state...  86.4 us

profile of v7, /device:TPU:0, one launch (start us, length us, event | category | flops | bytes accessed | tf_op | source)
XLA Modules:
  0.0 88.8 jit_solution(10467449106228117575)
XLA Ops:
  0.6 86.4 %line_reduce.1 = (f32[2,512,256]{2,1,0:T(8,128)S(1)}, f32[2,512,256]{2,1,0:T(8,128)S(1)}, f32[2,512,256]{2,1,0:T(8,128)S(1)}, f32[2,512,256]{2,1,0:T(8,128)S(1)}...) custom-call(s32[1,2]{1,0:T(1,128)} %refs_0_.1, f32[1,2]{1,0:T(1,128)} %refs_1_.1, s32[2]{0:T(128)} %refs_2_.1, ...), custom_call_target="tpu_custom_call" | custom-call | tf_op jit(solution)/shard_map/line_reduce/pallas_call | solution.py:555
  87.1 1.7 %update.1 = (f32[2,512,256]{2,1,0:T(8,128)}, f32[2,512,256]{2,1,0:T(8,128)}, f32[2,512,256]{2,1,0:T(8,128)}, f32[1,2]{1,0:T(1,128)}) custom-call(f32[2,512,256]{2,1,0:T(8,128)S(1)} %get-tuple-element.14.gradient, f32[2,512,256]{2,1,0:T(8,128)S(1)} %get-tuple-element.15.params, f32[2,512,256]{2,1,0:T(8,128)S(1)} %get-tuple-element.16.moment, ...), custom_call_target="tpu_custom_call" | custom-call | tf_op jit(solution)/shard_map/update/pallas_call | solution.py:587

commit v8 on v7

--- a/solution.py
+++ b/solution.py
@@ -82,11 +82,6 @@
     barrier = pltpu.get_barrier_semaphore()
     devices = 8 * n_mp
     place_in_all = dp * n_mp + mp
-
-    def away(i):
-        other_z, other_x, other_mp = z ^ (i // (2 * n_mp)), x ^ (i // n_mp % 2), mp ^ (i % n_mp)
-        other_dp = other_z * 2 + other_x
-        return other_dp * n_mp + other_mp, {"dp": other_dp, "mp": other_mp}
 
     def greet(sem, device):
         pl.semaphore_signal(sem, inc=1, device_id=device, device_id_type=MESH_ID)
@@ -449,11 +444,10 @@
         each(early, pieces, last)
         each(0, tail, last)
 
-    def share_square(i):
+    def share_square(target):
         return pltpu.make_async_remote_copy(
-            src_ref=st1.at[place_in_all], dst_ref=st1.at[place_in_all],
-            send_sem=st1_send, recv_sem=st1_recv,
-            device_id=away(i)[1], device_id_type=MESH_ID,
+            src_ref=st1.at[place_in_all], dst_ref=st1.at[place_in_all], send_sem=st1_send, recv_sem=st1_recv,
+            device_id={"dp": target // n_mp, "mp": target % n_mp}, device_id_type=MESH_ID,
         )
 
     def all_squares():
@@ -464,8 +458,8 @@
 
     folded = jnp.sum(square[...], axis=0, keepdims=True)
     st1[place_in_all] = sum(folded[:, i : i + LANES] for i in range(0, folded.shape[1], LANES))
-    for i in range(devices - 1, 0, -1):
-        share_square(i).start()
+    for target in range(devices):
+        pl.when(place_in_all != target)(lambda: share_square(target).start())
 
     @pl.when(place == 0)
     def _():

time: 88.9 us -> 88.9 us (level)
  no operation moved by 1% of the time
where the time goes in v8:
time: 88.9 us; the launch traced here: 88.8 us
  Pallas kernels  88.1 us (99%)
    pallas_call x1, Pallas kernels, line_body(): pl.pallas_call(kernel, name='line_reduce', out_shape=(state, state, state...  86.4 us

profile of v8, /device:TPU:0, one launch (start us, length us, event | category | flops | bytes accessed | tf_op | source)
XLA Modules:
  0.0 88.8 jit_solution(7700508159676970571)
XLA Ops:
  0.6 86.4 %line_reduce.1 = (f32[2,512,256]{2,1,0:T(8,128)S(1)}, f32[2,512,256]{2,1,0:T(8,128)S(1)}, f32[2,512,256]{2,1,0:T(8,128)S(1)}, f32[2,512,256]{2,1,0:T(8,128)S(1)}...) custom-call(s32[1,2]{1,0:T(1,128)} %refs_0_.1, f32[1,2]{1,0:T(1,128)} %refs_1_.1, s32[2]{0:T(128)} %refs_2_.1, ...), custom_call_target="tpu_custom_call" | custom-call | tf_op jit(solution)/shard_map/line_reduce/pallas_call | solution.py:549
  87.1 1.7 %update.1 = (f32[2,512,256]{2,1,0:T(8,128)}, f32[2,512,256]{2,1,0:T(8,128)}, f32[2,512,256]{2,1,0:T(8,128)}, f32[1,2]{1,0:T(1,128)}) custom-call(f32[2,512,256]{2,1,0:T(8,128)S(1)} %get-tuple-element.14.gradient, f32[2,512,256]{2,1,0:T(8,128)S(1)} %get-tuple-element.15.params, f32[2,512,256]{2,1,0:T(8,128)S(1)} %get-tuple-element.16.moment, ...), custom_call_target="tpu_custom_call" | custom-call | tf_op jit(solution)/shard_map/update/pallas_call | solution.py:581
